TPU v7x, 32 devices: a whole 2x2x4 slice. The times are simulated.
32 devices in a mesh: data: 4 (over z), cp: 8 (over y, x, core).
Axes of the slice: x: 2, y: 2, z: 4, core: 2. Of those that a mesh axis runs over, the one named last changes fastest.
Arguments:
- q: bfloat16 [4, 2048, 32, 128], P('data', 'cp'), parts along dimension 0
- k: bfloat16 [4, 2048, 32, 128], P('data', 'cp'), parts along dimension 0
- v: bfloat16 [4, 2048, 32, 128], P('data', 'cp'), parts along dimension 0
- o: bfloat16 [4, 2048, 32, 128], P('data', 'cp'), parts along dimension 0
- lse: float32 [4, 32, 2048], P('data', None, 'cp'), parts along dimension 0
- do: bfloat16 [4, 2048, 32, 128], P('data', 'cp'), parts along dimension 0
Outputs:
- output 1: bfloat16 [4, 2048, 32, 128], P('data', 'cp'), parts along dimension 0
- output 2: bfloat16 [4, 2048, 32, 128], P('data', 'cp'), parts along dimension 0
- output 3: bfloat16 [4, 2048, 32, 128], P('data', 'cp'), parts along dimension 0
There are 4 independent parts. A program takes and returns all parts, laid end to end along the dimension named above; each array names one.
All inputs are finite; a program needn't handle non-finite values.
Results may differ from a plain program's by a relative error of at most 0.001.
Values are sent between devices in bfloat16 or wider.
A program may use at most 1 GiB of HBM per device.

v0:
```python
import jax
import jax.numpy as jnp
from jax import lax
from jax.sharding import PartitionSpec as P

F32 = jnp.float32
BF16 = jnp.bfloat16


def _pair(q, do, lse, delta, k, v, mask, scale):
    s = jnp.einsum('bqhd,bkhd->bhqk', q, k, preferred_element_type=F32) * scale
    p = jnp.exp(s - lse[..., None])
    if mask is not None:
        p = jnp.where(mask, p, 0.0)
    dv = jnp.einsum('bhqk,bqhd->bkhd', p.astype(BF16), do, preferred_element_type=F32)
    dp = jnp.einsum('bqhd,bkhd->bhqk', do, v, preferred_element_type=F32)
    ds = (p * (dp - delta[..., None])).astype(BF16)
    dq = jnp.einsum('bhqk,bkhd->bqhd', ds, k, preferred_element_type=F32) * scale
    dk = jnp.einsum('bhqk,bqhd->bkhd', ds, q, preferred_element_type=F32) * scale
    return dq, dk, dv


def _same(q, do, lse, delta, k, v):
    c = q.shape[1] // 2
    scale = q.shape[-1] ** -0.5
    tri = jnp.tril(jnp.ones((c, c), bool))
    full = jnp.concatenate([jnp.ones((c, c), bool), tri], axis=1)
    dq0, dk0, dv0 = _pair(q[:, :c], do[:, :c], lse[..., :c], delta[..., :c], k[:, :c], v[:, :c], tri, scale)
    dq1, dk1, dv1 = _pair(q[:, c:], do[:, c:], lse[..., c:], delta[..., c:], k, v, full, scale)
    return jnp.concatenate([dq0, dq1], axis=1), dk1.at[:, :c].add(dk0), dv1.at[:, :c].add(dv0)


def _second_queries(q, do, lse, delta, k, v):
    c = q.shape[1] // 2
    scale = q.shape[-1] ** -0.5
    dq, dk, dv = _pair(q[:, c:], do[:, c:], lse[..., c:], delta[..., c:], k, v, None, scale)
    return jnp.concatenate([jnp.zeros_like(dq), dq], axis=1), dk, dv


def _first_keys(q, do, lse, delta, k, v):
    c = q.shape[1] // 2
    scale = q.shape[-1] ** -0.5
    dq, dk, dv = _pair(q, do, lse, delta, k[:, :c], v[:, :c], None, scale)
    return dq, jnp.concatenate([dk, jnp.zeros_like(dk)], axis=1), jnp.concatenate([dv, jnp.zeros_like(dv)], axis=1)


def solution(mesh):
    n = mesh.shape['cp']
    nxt = [(j, (j + 1) % n) for j in range(n)]
    spec = P('data', 'cp', None, None)
    lspec = P('data', None, 'cp')

    def local(q, k, v, o, lse, do):
        i = lax.axis_index('cp')
        delta = jnp.einsum('bqhd,bqhd->bhq', do, o, preferred_element_type=F32)
        dq, dk, dv = _same(q, do, lse, delta, k, v)
        qt, dot, lt, deltat = q, do, lse, delta
        for r in range(1, n):
            qt, dot, lt, deltat, dq = (lax.ppermute(x, 'cp', nxt) for x in (qt, dot, lt, deltat, dq))
            src = (i - r) % n
            ddq, ddk, ddv = lax.cond(src < i, _second_queries, _first_keys, qt, dot, lt, deltat, k, v)
            dq = dq + ddq
            dk = dk + ddk
            dv = dv + ddv
        dq = lax.ppermute(dq, 'cp', nxt)
        return dq.astype(BF16), dk.astype(BF16), dv.astype(BF16)

    return jax.shard_map(local, mesh=mesh, in_specs=(spec, spec, spec, spec, lspec, spec),
                         out_specs=(spec, spec, spec), check_vma=False)
```

profile of v0, /device:TPU:0, one launch (start us, length us, event | category | flops | bytes accessed | tf_op | source)
XLA Modules:
  0.0 907.6 jit_solution(8183271769606580474)
XLA Ops:
  0.7 3.9 copy.37
  4.5 2.1 copy.39
  9.7 2.6 fusion.308
  13.0 4.7 multiply_convert_fusion.14
  19.1 2.7 exponential_select_fusion.1
  21.9 2.9 multiply_convert_fusion.15
  26.6 2.5 pad_maximum_fusion
  29.6 2.6 collective-permute-start.1
  33.8 90.1 %collective-permute-done.2 = f32[1,32,256]{2,1,0:T(8,128)S(1)} collective-permute-done((f32[1,32,256]{2,1,0:T(8,128)S(1)}, f32[1,32,256]{2,1,0:T(8,128)S(1)}, u32[]{:S(2)}, u32[]{:S(2)}) %collective-permute-start.2) | collective-permute-done | bytes 32800 | tf_op jit(solution)/shard_map/ppermute | solution.py:59
  124.3 26.9 %conditional.7 = (f32[1,256,32,128]{3,1,2,0:T(8,128)S(1)}, f32[1,256,32,128]{3,1,2,0:T(8,128)S(1)}, f32[1,256,32,128]{3,1,2,0:T(8,128)S(1)}) conditional(s32[]{:T(128)} %convert_element_type.160, (bf16[1,256,32,128]{3,1,2,0:T(8,128)(2,1)}, bf16[1,256,32,128]{3,2,1,0:T(8,128)(2,1)S(1)}, f32[1,32,256]{2,1,0:T(8,128)S(1)}, ...), branch_computations={%region_0.1_spmd, %region_1.2_spmd} | conditional | flops 1352138752 | bytes 68255800 | solution.py:61
  125.4 2.4 fusion.7
  128.7 3.7 multiply_convert_fusion
  133.1 2.4 multiply_bitcast_fusion.1
  136.0 4.7 fusion.13
  151.3 7.8 add.158
  160.2 93.0 %collective-permute-done.7 = f32[1,32,256]{2,1,0:T(8,128)S(1)} collective-permute-done((f32[1,32,256]{2,1,0:T(8,128)S(1)}, f32[1,32,256]{2,1,0:T(8,128)S(1)}, u32[]{:S(2)}, u32[]{:S(2)}) %collective-permute-start.7) | collective-permute-done | bytes 32800 | tf_op jit(solution)/shard_map/ppermute | solution.py:59
  253.5 16.6 %conditional.8 = (f32[1,256,32,128]{3,1,2,0:T(8,128)S(1)}, f32[1,256,32,128]{3,1,2,0:T(8,128)S(1)}, f32[1,256,32,128]{3,1,2,0:T(8,128)S(1)}) conditional(s32[]{:T(128)} %convert_element_type.161, (bf16[1,256,32,128]{3,1,2,0:T(8,128)(2,1)}, bf16[1,256,32,128]{3,2,1,0:T(8,128)(2,1)S(1)}, f32[1,32,256]{2,1,0:T(8,128)S(1)}, ...), branch_computations={%region_2.3_spmd, %region_3.4_spmd} | conditional | flops 1352138752 | bytes 68255800 | solution.py:61
  254.4 2.4 fusion.49
  257.6 3.7 multiply_convert_fusion.2
  262.0 2.4 multiply_bitcast_fusion.5
  264.9 4.7 fusion.55
  270.1 7.7 add.160
  278.1 93.8 %collective-permute-done.12 = f32[1,32,256]{2,1,0:T(8,128)S(1)} collective-permute-done((f32[1,32,256]{2,1,0:T(8,128)S(1)}, f32[1,32,256]{2,1,0:T(8,128)S(1)}, u32[]{:S(2)}, u32[]{:S(2)}) %collective-permute-start.12) | collective-permute-done | bytes 32800 | tf_op jit(solution)/shard_map/ppermute | solution.py:59
  372.3 17.1 %conditional.9 = (f32[1,256,32,128]{3,1,2,0:T(8,128)S(1)}, f32[1,256,32,128]{3,1,2,0:T(8,128)S(1)}, f32[1,256,32,128]{3,1,2,0:T(8,128)S(1)}) conditional(s32[]{:T(128)} %convert_element_type.162, (bf16[1,256,32,128]{3,1,2,0:T(8,128)(2,1)}, bf16[1,256,32,128]{3,2,1,0:T(8,128)(2,1)S(1)}, f32[1,32,256]{2,1,0:T(8,128)S(1)}, ...), branch_computations={%region_4.5_spmd, %region_5.6_spmd} | conditional | flops 1352138752 | bytes 68255800 | solution.py:61
  373.6 2.4 fusion.91
  376.8 3.7 multiply_convert_fusion.4
  381.2 2.4 multiply_bitcast_fusion.9
  384.1 4.7 fusion.97
  389.5 7.7 add.162
  397.5 93.8 %collective-permute-done.17 = f32[1,32,256]{2,1,0:T(8,128)S(1)} collective-permute-done((f32[1,32,256]{2,1,0:T(8,128)S(1)}, f32[1,32,256]{2,1,0:T(8,128)S(1)}, u32[]{:S(2)}, u32[]{:S(2)}) %collective-permute-start.17) | collective-permute-done | bytes 32800 | tf_op jit(solution)/shard_map/ppermute | solution.py:59
  491.7 16.6 %conditional.10 = (f32[1,256,32,128]{3,1,2,0:T(8,128)S(1)}, f32[1,256,32,128]{3,1,2,0:T(8,128)S(1)}, f32[1,256,32,128]{3,1,2,0:T(8,128)S(1)}) conditional(s32[]{:T(128)} %convert_element_type.163, (bf16[1,256,32,128]{3,1,2,0:T(8,128)(2,1)}, bf16[1,256,32,128]{3,2,1,0:T(8,128)(2,1)S(1)}, f32[1,32,256]{2,1,0:T(8,128)S(1)}, ...), branch_computations={%region_6.7_spmd, %region_7.8_spmd} | conditional | flops 1352138752 | bytes 68255800 | solution.py:61
  492.5 2.4 fusion.133
  495.8 3.7 multiply_convert_fusion.6
  500.2 2.4 multiply_bitcast_fusion.13
  503.1 4.7 fusion.139
  508.3 7.7 add.164
  516.3 93.8 %collective-permute-done.22 = f32[1,32,256]{2,1,0:T(8,128)S(1)} collective-permute-done((f32[1,32,256]{2,1,0:T(8,128)S(1)}, f32[1,32,256]{2,1,0:T(8,128)S(1)}, u32[]{:S(2)}, u32[]{:S(2)}) %collective-permute-start.22) | collective-permute-done | bytes 32800 | tf_op jit(solution)/shard_map/ppermute | solution.py:59
  610.5 17.2 %conditional.11 = (f32[1,256,32,128]{3,1,2,0:T(8,128)S(1)}, f32[1,256,32,128]{3,1,2,0:T(8,128)S(1)}, f32[1,256,32,128]{3,1,2,0:T(8,128)S(1)}) conditional(s32[]{:T(128)} %convert_element_type.164, (bf16[1,256,32,128]{3,1,2,0:T(8,128)(2,1)}, bf16[1,256,32,128]{3,2,1,0:T(8,128)(2,1)S(1)}, f32[1,32,256]{2,1,0:T(8,128)S(1)}, ...), branch_computations={%region_8.9_spmd, %region_9.10_spmd} | conditional | flops 1352138752 | bytes 68255800 | solution.py:61
  611.5 2.4 fusion.175
  614.8 3.7 multiply_convert_fusion.8
  619.2 2.4 multiply_bitcast_fusion.17
  622.1 4.7 fusion.181
  627.7 7.7 add.166
  635.7 93.8 %collective-permute-done.27 = f32[1,32,256]{2,1,0:T(8,128)S(1)} collective-permute-done((f32[1,32,256]{2,1,0:T(8,128)S(1)}, f32[1,32,256]{2,1,0:T(8,128)S(1)}, u32[]{:S(2)}, u32[]{:S(2)}) %collective-permute-start.27) | collective-permute-done | bytes 32800 | tf_op jit(solution)/shard_map/ppermute | solution.py:59
  729.9 16.7 %conditional.12 = (f32[1,256,32,128]{3,1,2,0:T(8,128)S(1)}, f32[1,256,32,128]{3,1,2,0:T(8,128)S(1)}, f32[1,256,32,128]{3,1,2,0:T(8,128)S(1)}) conditional(s32[]{:T(128)} %convert_element_type.165, (bf16[1,256,32,128]{3,1,2,0:T(8,128)(2,1)}, bf16[1,256,32,128]{3,2,1,0:T(8,128)(2,1)S(1)}, f32[1,32,256]{2,1,0:T(8,128)S(1)}, ...), branch_computations={%region_10.11_spmd, %region_11.12_spmd} | conditional | flops 1352138752 | bytes 68255800 | solution.py:61
  730.7 2.4 fusion.217
  734.0 3.7 multiply_convert_fusion.10
  738.4 2.4 multiply_bitcast_fusion.21
  741.3 4.7 fusion.223
  746.7 7.8 add.168
  754.6 3.0 fusion.296
  759.2 4.1 multiply_bitcast_fusion.28
  767.3 3.8 fusion.300
  771.2 77.4 %collective-permute-done.32 = f32[1,32,256]{2,1,0:T(8,128)S(1)} collective-permute-done((f32[1,32,256]{2,1,0:T(8,128)S(1)}, f32[1,32,256]{2,1,0:T(8,128)S(1)}, u32[]{:S(2)}, u32[]{:S(2)}) %collective-permute-start.32) | collective-permute-done | bytes 32800 | tf_op jit(solution)/shard_map/ppermute | solution.py:59
  849.0 16.9 %conditional.13 = (f32[1,256,32,128]{3,1,2,0:T(8,128)S(1)}, f32[1,256,32,128]{3,1,2,0:T(8,128)S(1)}, f32[1,256,32,128]{3,1,2,0:T(8,128)S(1)}) conditional(s32[]{:T(128)} %convert_element_type.166, (bf16[1,256,32,128]{3,1,2,0:T(8,128)(2,1)}, bf16[1,256,32,128]{3,2,1,0:T(8,128)(2,1)S(1)}, f32[1,32,256]{2,1,0:T(8,128)S(1)}, ...), branch_computations={%region_12.13_spmd, %region_13.14_spmd} | conditional | flops 1352138752 | bytes 68255800 | solution.py:61
  850.0 2.4 fusion.259
  853.3 3.7 multiply_convert_fusion.12
  857.6 2.4 multiply_bitcast_fusion.25
  860.5 4.7 fusion.265
  865.9 7.1 add.170
  873.1 22.9 %add_convert_fusion = (bf16[1,256,32,128]{3,1,2,0:T(8,128)(2,1)S(1)}, bf16[1,256,32,128]{3,1,2,0:T(8,128)(2,1)}) fusion(f32[1,256,32,128]{3,1,2,0:T(8,128)} %copy-done.31, f32[1,256,32,128]{3,1,2,0:T(8,128)} %copy-done.29, f32[1,256,32,128]{3,1,2,0:T(8,128)} %copy-done.28, f32[1,256,32,128]{3,1,2,0:T(8,128)} %copy-done.27, ...), kind=kLoop, calls=%fused_computation.318 | loop fusion | flops 16777216 | bytes 71303168 | tf_op jit(solution)/shard_map/convert_element_type | solution.py:66
  896.0 4.3 copy.81
  900.2 2.7 copy.82
  902.9 4.3 copy.80
  (191 shorter events, 42.9 us)
Async XLA Ops:
  0.7 3.9 copy-start.40
  8.3 4.0 copy-start.44
  12.3 5.4 copy-start.32
  21.8 2.9 copy-start.38
  29.1 122.2 %collective-permute-start = (f32[1,256,32,128]{3,1,2,0:T(8,128)}, f32[1,256,32,128]{3,1,2,0:T(8,128)}, u32[]{:S(2)}, u32[]{:S(2)}) collective-permute-start(f32[1,256,32,128]{3,1,2,0:T(8,128)} %pad_maximum_fusion), channel_id=1, source_target_pairs={{0,1},{1,2},{2,3},{3,4},{4,5},{5,6},{6,7},{7,0},{8,9},{9,10},{10,1... | collective-permute-start | bytes 12582920 | tf_op jit(solution)/shard_map/ppermute | solution.py:59
  29.6 94.7 %collective-permute-start.1 = (bf16[1,256,32,128]{3,1,2,0:T(8,128)(2,1)}, bf16[1,256,32,128]{3,1,2,0:T(8,128)(2,1)}, u32[]{:S(2)}, u32[]{:S(2)}) collective-permute-start(bf16[1,256,32,128]{3,1,2,0:T(8,128)(2,1)} %copy.37), channel_id=1, source_target_pairs={{0,1},{1,2},{2,3},{3,4},{4,5},{5,6},{6,7},{7,0},{8,9},{9,10},{10,1... | collective-permute-start | bytes 6291464 | tf_op jit(solution)/shard_map/ppermute | solution.py:59
  32.2 92.1 %collective-permute-start.3 = (bf16[1,256,32,128]{3,1,2,0:T(8,128)(2,1)}, bf16[1,256,32,128]{3,1,2,0:T(8,128)(2,1)}, u32[]{:S(2)}, u32[]{:S(2)}) collective-permute-start(bf16[1,256,32,128]{3,1,2,0:T(8,128)(2,1)} %copy.39), channel_id=1, source_target_pairs={{0,1},{1,2},{2,3},{3,4},{4,5},{5,6},{6,7},{7,0},{8,9},{9,10},{10,1... | collective-permute-start | bytes 6291464 | tf_op jit(solution)/shard_map/ppermute | solution.py:59
  32.2 91.7 %collective-permute-start.2 = (f32[1,32,256]{2,1,0:T(8,128)S(1)}, f32[1,32,256]{2,1,0:T(8,128)S(1)}, u32[]{:S(2)}, u32[]{:S(2)}) collective-permute-start(f32[1,32,256]{2,1,0:T(8,128)S(1)} %copy-done.46), channel_id=1, source_target_pairs={{0,1},{1,2},{2,3},{3,4},{4,5},{5,6},{6,7},{7,0},{8,9},{9,10},{10,1... | collective-permute-start | bytes 98312 | tf_op jit(solution)/shard_map/ppermute | solution.py:59
  33.8 90.5 %collective-permute-start.4 = (f32[1,32,256]{2,1,0:T(8,128)S(1)}, f32[1,32,256]{2,1,0:T(8,128)S(1)}, u32[]{:S(2)}, u32[]{:S(2)}) collective-permute-start(f32[1,32,256]{2,1,0:T(8,128)S(1)} %bitcast.711), channel_id=1, source_target_pairs={{0,1},{1,2},{2,3},{3,4},{4,5},{5,6},{6,7},{7,0},{8,9},{9,10},{10,1... | collective-permute-start | bytes 98312 | tf_op jit(solution)/shard_map/ppermute | solution.py:59
  125.4 2.5 copy-start.2
  151.2 7.8 copy-start.16
  151.2 7.8 copy-start.24
  159.1 111.1 %collective-permute-start.5 = (f32[1,256,32,128]{3,1,2,0:T(8,128)}, f32[1,256,32,128]{3,1,2,0:T(8,128)}, u32[]{:S(2)}, u32[]{:S(2)}) collective-permute-start(f32[1,256,32,128]{3,1,2,0:T(8,128)} %add.158), channel_id=1, source_target_pairs={{0,1},{1,2},{2,3},{3,4},{4,5},{5,6},{6,7},{7,0},{8,9},{9,10},{10,1... | collective-permute-start | bytes 12582920 | tf_op jit(solution)/shard_map/ppermute | solution.py:59
  159.1 94.5 %collective-permute-start.6 = (bf16[1,256,32,128]{3,1,2,0:T(8,128)(2,1)}, bf16[1,256,32,128]{3,1,2,0:T(8,128)(2,1)}, u32[]{:S(2)}, u32[]{:S(2)}) collective-permute-start(bf16[1,256,32,128]{3,1,2,0:T(8,128)(2,1)} %collective-permute-done.1), channel_id=1, source_target_pairs={{0,1},{1,2},{2,3},{3,4},{4,5},{5,6},{6,7},{7,0},{8,9},{9,10},{10,1... | collective-permute-start | bytes 6291464 | tf_op jit(solution)/shard_map/ppermute | solution.py:59
  159.1 94.4 %collective-permute-start.8 = (bf16[1,256,32,128]{3,1,2,0:T(8,128)(2,1)}, bf16[1,256,32,128]{3,1,2,0:T(8,128)(2,1)}, u32[]{:S(2)}, u32[]{:S(2)}) collective-permute-start(bf16[1,256,32,128]{3,1,2,0:T(8,128)(2,1)} %collective-permute-done.3), channel_id=1, source_target_pairs={{0,1},{1,2},{2,3},{3,4},{4,5},{5,6},{6,7},{7,0},{8,9},{9,10},{10,1... | collective-permute-start | bytes 6291464 | tf_op jit(solution)/shard_map/ppermute | solution.py:59
  159.2 94.0 %collective-permute-start.7 = (f32[1,32,256]{2,1,0:T(8,128)S(1)}, f32[1,32,256]{2,1,0:T(8,128)S(1)}, u32[]{:S(2)}, u32[]{:S(2)}) collective-permute-start(f32[1,32,256]{2,1,0:T(8,128)S(1)} %collective-permute-done.2), channel_id=1, source_target_pairs={{0,1},{1,2},{2,3},{3,4},{4,5},{5,6},{6,7},{7,0},{8,9},{9,10},{10,1... | collective-permute-start | bytes 98312 | tf_op jit(solution)/shard_map/ppermute | solution.py:59
  160.1 93.4 %collective-permute-start.9 = (f32[1,32,256]{2,1,0:T(8,128)S(1)}, f32[1,32,256]{2,1,0:T(8,128)S(1)}, u32[]{:S(2)}, u32[]{:S(2)}) collective-permute-start(f32[1,32,256]{2,1,0:T(8,128)S(1)} %collective-permute-done.4), channel_id=1, source_target_pairs={{0,1},{1,2},{2,3},{3,4},{4,5},{5,6},{6,7},{7,0},{8,9},{9,10},{10,1... | collective-permute-start | bytes 98312 | tf_op jit(solution)/shard_map/ppermute | solution.py:59
  254.3 2.5 copy-start.4
  270.1 7.7 copy-start.18
  270.1 7.7 copy-start.25
  277.8 111.6 %collective-permute-start.10 = (f32[1,256,32,128]{3,1,2,0:T(8,128)}, f32[1,256,32,128]{3,1,2,0:T(8,128)}, u32[]{:S(2)}, u32[]{:S(2)}) collective-permute-start(f32[1,256,32,128]{3,1,2,0:T(8,128)} %add.160), channel_id=1, source_target_pairs={{0,1},{1,2},{2,3},{3,4},{4,5},{5,6},{6,7},{7,0},{8,9},{9,10},{10,1... | collective-permute-start | bytes 12582920 | tf_op jit(solution)/shard_map/ppermute | solution.py:59
  277.9 94.5 %collective-permute-start.11 = (bf16[1,256,32,128]{3,1,2,0:T(8,128)(2,1)}, bf16[1,256,32,128]{3,1,2,0:T(8,128)(2,1)}, u32[]{:S(2)}, u32[]{:S(2)}) collective-permute-start(bf16[1,256,32,128]{3,1,2,0:T(8,128)(2,1)} %collective-permute-done.6), channel_id=1, source_target_pairs={{0,1},{1,2},{2,3},{3,4},{4,5},{5,6},{6,7},{7,0},{8,9},{9,10},{10,1... | collective-permute-start | bytes 6291464 | tf_op jit(solution)/shard_map/ppermute | solution.py:59
  277.9 94.4 %collective-permute-start.13 = (bf16[1,256,32,128]{3,1,2,0:T(8,128)(2,1)}, bf16[1,256,32,128]{3,1,2,0:T(8,128)(2,1)}, u32[]{:S(2)}, u32[]{:S(2)}) collective-permute-start(bf16[1,256,32,128]{3,1,2,0:T(8,128)(2,1)} %collective-permute-done.8), channel_id=1, source_target_pairs={{0,1},{1,2},{2,3},{3,4},{4,5},{5,6},{6,7},{7,0},{8,9},{9,10},{10,1... | collective-permute-start | bytes 6291464 | tf_op jit(solution)/shard_map/ppermute | solution.py:59
  278.0 94.0 %collective-permute-start.12 = (f32[1,32,256]{2,1,0:T(8,128)S(1)}, f32[1,32,256]{2,1,0:T(8,128)S(1)}, u32[]{:S(2)}, u32[]{:S(2)}) collective-permute-start(f32[1,32,256]{2,1,0:T(8,128)S(1)} %collective-permute-done.7), channel_id=1, source_target_pairs={{0,1},{1,2},{2,3},{3,4},{4,5},{5,6},{6,7},{7,0},{8,9},{9,10},{10,1... | collective-permute-start | bytes 98312 | tf_op jit(solution)/shard_map/ppermute | solution.py:59
  278.1 94.3 %collective-permute-start.14 = (f32[1,32,256]{2,1,0:T(8,128)S(1)}, f32[1,32,256]{2,1,0:T(8,128)S(1)}, u32[]{:S(2)}, u32[]{:S(2)}) collective-permute-start(f32[1,32,256]{2,1,0:T(8,128)S(1)} %collective-permute-done.9), channel_id=1, source_target_pairs={{0,1},{1,2},{2,3},{3,4},{4,5},{5,6},{6,7},{7,0},{8,9},{9,10},{10,1... | collective-permute-start | bytes 98312 | tf_op jit(solution)/shard_map/ppermute | solution.py:59
  389.5 7.8 copy-start.19
  389.5 7.8 copy-start.26
  397.2 111.1 %collective-permute-start.15 = (f32[1,256,32,128]{3,1,2,0:T(8,128)}, f32[1,256,32,128]{3,1,2,0:T(8,128)}, u32[]{:S(2)}, u32[]{:S(2)}) collective-permute-start(f32[1,256,32,128]{3,1,2,0:T(8,128)} %add.162), channel_id=1, source_target_pairs={{0,1},{1,2},{2,3},{3,4},{4,5},{5,6},{6,7},{7,0},{8,9},{9,10},{10,1... | collective-permute-start | bytes 12582920 | tf_op jit(solution)/shard_map/ppermute | solution.py:59
  397.2 94.5 %collective-permute-start.16 = (bf16[1,256,32,128]{3,1,2,0:T(8,128)(2,1)}, bf16[1,256,32,128]{3,1,2,0:T(8,128)(2,1)}, u32[]{:S(2)}, u32[]{:S(2)}) collective-permute-start(bf16[1,256,32,128]{3,1,2,0:T(8,128)(2,1)} %collective-permute-done.11), channel_id=1, source_target_pairs={{0,1},{1,2},{2,3},{3,4},{4,5},{5,6},{6,7},{7,0},{8,9},{9,10},{10,1... | collective-permute-start | bytes 6291464 | tf_op jit(solution)/shard_map/ppermute | solution.py:59
  397.3 94.4 %collective-permute-start.18 = (bf16[1,256,32,128]{3,1,2,0:T(8,128)(2,1)}, bf16[1,256,32,128]{3,1,2,0:T(8,128)(2,1)}, u32[]{:S(2)}, u32[]{:S(2)}) collective-permute-start(bf16[1,256,32,128]{3,1,2,0:T(8,128)(2,1)} %collective-permute-done.13), channel_id=1, source_target_pairs={{0,1},{1,2},{2,3},{3,4},{4,5},{5,6},{6,7},{7,0},{8,9},{9,10},{10,1... | collective-permute-start | bytes 6291464 | tf_op jit(solution)/shard_map/ppermute | solution.py:59
  397.4 94.0 %collective-permute-start.17 = (f32[1,32,256]{2,1,0:T(8,128)S(1)}, f32[1,32,256]{2,1,0:T(8,128)S(1)}, u32[]{:S(2)}, u32[]{:S(2)}) collective-permute-start(f32[1,32,256]{2,1,0:T(8,128)S(1)} %collective-permute-done.12), channel_id=1, source_target_pairs={{0,1},{1,2},{2,3},{3,4},{4,5},{5,6},{6,7},{7,0},{8,9},{9,10},{10,1... | collective-permute-start | bytes 98312 | tf_op jit(solution)/shard_map/ppermute | solution.py:59
  397.4 94.3 %collective-permute-start.19 = (f32[1,32,256]{2,1,0:T(8,128)S(1)}, f32[1,32,256]{2,1,0:T(8,128)S(1)}, u32[]{:S(2)}, u32[]{:S(2)}) collective-permute-start(f32[1,32,256]{2,1,0:T(8,128)S(1)} %collective-permute-done.14), channel_id=1, source_target_pairs={{0,1},{1,2},{2,3},{3,4},{4,5},{5,6},{6,7},{7,0},{8,9},{9,10},{10,1... | collective-permute-start | bytes 98312 | tf_op jit(solution)/shard_map/ppermute | solution.py:59
  508.3 7.7 copy-start.20
  508.3 7.7 copy-start.27
  516.0 111.7 %collective-permute-start.20 = (f32[1,256,32,128]{3,1,2,0:T(8,128)}, f32[1,256,32,128]{3,1,2,0:T(8,128)}, u32[]{:S(2)}, u32[]{:S(2)}) collective-permute-start(f32[1,256,32,128]{3,1,2,0:T(8,128)} %add.164), channel_id=1, source_target_pairs={{0,1},{1,2},{2,3},{3,4},{4,5},{5,6},{6,7},{7,0},{8,9},{9,10},{10,1... | collective-permute-start | bytes 12582920 | tf_op jit(solution)/shard_map/ppermute | solution.py:59
  516.0 94.5 %collective-permute-start.21 = (bf16[1,256,32,128]{3,1,2,0:T(8,128)(2,1)}, bf16[1,256,32,128]{3,1,2,0:T(8,128)(2,1)}, u32[]{:S(2)}, u32[]{:S(2)}) collective-permute-start(bf16[1,256,32,128]{3,1,2,0:T(8,128)(2,1)} %collective-permute-done.16), channel_id=1, source_target_pairs={{0,1},{1,2},{2,3},{3,4},{4,5},{5,6},{6,7},{7,0},{8,9},{9,10},{10,1... | collective-permute-start | bytes 6291464 | tf_op jit(solution)/shard_map/ppermute | solution.py:59
  516.1 94.4 %collective-permute-start.23 = (bf16[1,256,32,128]{3,1,2,0:T(8,128)(2,1)}, bf16[1,256,32,128]{3,1,2,0:T(8,128)(2,1)}, u32[]{:S(2)}, u32[]{:S(2)}) collective-permute-start(bf16[1,256,32,128]{3,1,2,0:T(8,128)(2,1)} %collective-permute-done.18), channel_id=1, source_target_pairs={{0,1},{1,2},{2,3},{3,4},{4,5},{5,6},{6,7},{7,0},{8,9},{9,10},{10,1... | collective-permute-start | bytes 6291464 | tf_op jit(solution)/shard_map/ppermute | solution.py:59
  516.1 94.0 %collective-permute-start.22 = (f32[1,32,256]{2,1,0:T(8,128)S(1)}, f32[1,32,256]{2,1,0:T(8,128)S(1)}, u32[]{:S(2)}, u32[]{:S(2)}) collective-permute-start(f32[1,32,256]{2,1,0:T(8,128)S(1)} %collective-permute-done.17), channel_id=1, source_target_pairs={{0,1},{1,2},{2,3},{3,4},{4,5},{5,6},{6,7},{7,0},{8,9},{9,10},{10,1... | collective-permute-start | bytes 98312 | tf_op jit(solution)/shard_map/ppermute | solution.py:59
  516.2 94.3 %collective-permute-start.24 = (f32[1,32,256]{2,1,0:T(8,128)S(1)}, f32[1,32,256]{2,1,0:T(8,128)S(1)}, u32[]{:S(2)}, u32[]{:S(2)}) collective-permute-start(f32[1,32,256]{2,1,0:T(8,128)S(1)} %collective-permute-done.19), channel_id=1, source_target_pairs={{0,1},{1,2},{2,3},{3,4},{4,5},{5,6},{6,7},{7,0},{8,9},{9,10},{10,1... | collective-permute-start | bytes 98312 | tf_op jit(solution)/shard_map/ppermute | solution.py:59
  627.7 7.8 copy-start.21
  627.7 7.8 copy-start.28
  635.4 111.2 %collective-permute-start.25 = (f32[1,256,32,128]{3,1,2,0:T(8,128)}, f32[1,256,32,128]{3,1,2,0:T(8,128)}, u32[]{:S(2)}, u32[]{:S(2)}) collective-permute-start(f32[1,256,32,128]{3,1,2,0:T(8,128)} %add.166), channel_id=1, source_target_pairs={{0,1},{1,2},{2,3},{3,4},{4,5},{5,6},{6,7},{7,0},{8,9},{9,10},{10,1... | collective-permute-start | bytes 12582920 | tf_op jit(solution)/shard_map/ppermute | solution.py:59
  635.4 94.5 %collective-permute-start.26 = (bf16[1,256,32,128]{3,1,2,0:T(8,128)(2,1)}, bf16[1,256,32,128]{3,1,2,0:T(8,128)(2,1)}, u32[]{:S(2)}, u32[]{:S(2)}) collective-permute-start(bf16[1,256,32,128]{3,1,2,0:T(8,128)(2,1)} %collective-permute-done.21), channel_id=1, source_target_pairs={{0,1},{1,2},{2,3},{3,4},{4,5},{5,6},{6,7},{7,0},{8,9},{9,10},{10,1... | collective-permute-start | bytes 6291464 | tf_op jit(solution)/shard_map/ppermute | solution.py:59
  635.5 94.4 %collective-permute-start.28 = (bf16[1,256,32,128]{3,1,2,0:T(8,128)(2,1)}, bf16[1,256,32,128]{3,1,2,0:T(8,128)(2,1)}, u32[]{:S(2)}, u32[]{:S(2)}) collective-permute-start(bf16[1,256,32,128]{3,1,2,0:T(8,128)(2,1)} %collective-permute-done.23), channel_id=1, source_target_pairs={{0,1},{1,2},{2,3},{3,4},{4,5},{5,6},{6,7},{7,0},{8,9},{9,10},{10,1... | collective-permute-start | bytes 6291464 | tf_op jit(solution)/shard_map/ppermute | solution.py:59
  635.6 94.0 %collective-permute-start.27 = (f32[1,32,256]{2,1,0:T(8,128)S(1)}, f32[1,32,256]{2,1,0:T(8,128)S(1)}, u32[]{:S(2)}, u32[]{:S(2)}) collective-permute-start(f32[1,32,256]{2,1,0:T(8,128)S(1)} %collective-permute-done.22), channel_id=1, source_target_pairs={{0,1},{1,2},{2,3},{3,4},{4,5},{5,6},{6,7},{7,0},{8,9},{9,10},{10,1... | collective-permute-start | bytes 98312 | tf_op jit(solution)/shard_map/ppermute | solution.py:59
  635.6 94.3 %collective-permute-start.29 = (f32[1,32,256]{2,1,0:T(8,128)S(1)}, f32[1,32,256]{2,1,0:T(8,128)S(1)}, u32[]{:S(2)}, u32[]{:S(2)}) collective-permute-start(f32[1,32,256]{2,1,0:T(8,128)S(1)} %collective-permute-done.24), channel_id=1, source_target_pairs={{0,1},{1,2},{2,3},{3,4},{4,5},{5,6},{6,7},{7,0},{8,9},{9,10},{10,1... | collective-permute-start | bytes 98312 | tf_op jit(solution)/shard_map/ppermute | solution.py:59
  730.7 2.5 copy-start.12
  746.7 7.8 copy-start.22
  746.7 7.8 copy-start.29
  746.7 7.9 copy-start.33
  746.7 7.9 copy-start.43
  746.7 7.9 copy-start.45
  754.5 111.4 %collective-permute-start.30 = (f32[1,256,32,128]{3,1,2,0:T(8,128)}, f32[1,256,32,128]{3,1,2,0:T(8,128)}, u32[]{:S(2)}, u32[]{:S(2)}) collective-permute-start(f32[1,256,32,128]{3,1,2,0:T(8,128)} %add.168), channel_id=1, source_target_pairs={{0,1},{1,2},{2,3},{3,4},{4,5},{5,6},{6,7},{7,0},{8,9},{9,10},{10,1... | collective-permute-start | bytes 12582920 | tf_op jit(solution)/shard_map/ppermute | solution.py:59
  754.5 94.5 %collective-permute-start.31 = (bf16[1,256,32,128]{3,1,2,0:T(8,128)(2,1)}, bf16[1,256,32,128]{3,1,2,0:T(8,128)(2,1)}, u32[]{:S(2)}, u32[]{:S(2)}) collective-permute-start(bf16[1,256,32,128]{3,1,2,0:T(8,128)(2,1)} %collective-permute-done.26), channel_id=1, source_target_pairs={{0,1},{1,2},{2,3},{3,4},{4,5},{5,6},{6,7},{7,0},{8,9},{9,10},{10,1... | collective-permute-start | bytes 6291464 | tf_op jit(solution)/shard_map/ppermute | solution.py:59
  754.6 94.4 %collective-permute-start.33 = (bf16[1,256,32,128]{3,1,2,0:T(8,128)(2,1)}, bf16[1,256,32,128]{3,1,2,0:T(8,128)(2,1)}, u32[]{:S(2)}, u32[]{:S(2)}) collective-permute-start(bf16[1,256,32,128]{3,1,2,0:T(8,128)(2,1)} %collective-permute-done.28), channel_id=1, source_target_pairs={{0,1},{1,2},{2,3},{3,4},{4,5},{5,6},{6,7},{7,0},{8,9},{9,10},{10,1... | collective-permute-start | bytes 6291464 | tf_op jit(solution)/shard_map/ppermute | solution.py:59
  759.2 4.2 copy-start.39
  763.4 4.0 copy-start.35
  767.3 81.3 %collective-permute-start.32 = (f32[1,32,256]{2,1,0:T(8,128)S(1)}, f32[1,32,256]{2,1,0:T(8,128)S(1)}, u32[]{:S(2)}, u32[]{:S(2)}) collective-permute-start(f32[1,32,256]{2,1,0:T(8,128)S(1)} %collective-permute-done.27), channel_id=1, source_target_pairs={{0,1},{1,2},{2,3},{3,4},{4,5},{5,6},{6,7},{7,0},{8,9},{9,10},{10,1... | collective-permute-start | bytes 98312 | tf_op jit(solution)/shard_map/ppermute | solution.py:59
  767.3 81.6 %collective-permute-start.34 = (f32[1,32,256]{2,1,0:T(8,128)S(1)}, f32[1,32,256]{2,1,0:T(8,128)S(1)}, u32[]{:S(2)}, u32[]{:S(2)}) collective-permute-start(f32[1,32,256]{2,1,0:T(8,128)S(1)} %collective-permute-done.29), channel_id=1, source_target_pairs={{0,1},{1,2},{2,3},{3,4},{4,5},{5,6},{6,7},{7,0},{8,9},{9,10},{10,1... | collective-permute-start | bytes 98312 | tf_op jit(solution)/shard_map/ppermute | solution.py:59
  850.0 2.5 copy-start.14
  865.9 7.2 copy-start.23
  865.9 7.2 copy-start.31
  865.9 7.2 copy-start.17
  873.1 29.8 %collective-permute-start.35 = (bf16[1,256,32,128]{3,1,2,0:T(8,128)(2,1)}, bf16[1,256,32,128]{3,1,2,0:T(8,128)(2,1)}, u32[]{:S(2)}, u32[]{:S(2)}) collective-permute-start(bf16[1,256,32,128]{3,1,2,0:T(8,128)(2,1)} %add.170), channel_id=1, source_target_pairs={{0,1},{1,2},{2,3},{3,4},{4,5},{5,6},{6,7},{7,0},{8,9},{9,10},{10,1... | collective-permute-start | bytes 6291464 | tf_op jit(solution)/shard_map/ppermute | solution.py:65
  (12 other events, 20.9 us)
where the time goes:
time: 916 us; the launch traced here: 908 us
  waiting for transfers between devices  638 us (70%)
  matrix products  125 us (14%)
  other arithmetic  80.1 us (9%)
  local copies, waits for them, and re-layouts  43.1 us (5%)
  loops' own time  12.6 us (1%)
    ppermute x35, waiting for transfers between devices, local(): lax.ppermute(x, 'cp', nxt)  638 us
    add x7, other arithmetic, local(): dq = dq + ddq  53.5 us
    dot_general x9, matrix products, _pair(): jnp.einsum('bhqk,bqhd->bkhd', p.astype(BF16), do, preferred_element_type=...  37.4 us
    dot_general x9, matrix products, _pair(): dp = jnp.einsum('bqhd,bkhd->bhqk', do, v, preferred_element_type=F32)  33.2 us
    dot_general x9, matrix products, _pair(): jnp.einsum('bhqk,bqhd->bkhd', ds, q, preferred_element_type=F32) * scale  24.5 us
    unnamed x72, local copies, waits for them, and re-layouts  24.2 us
    convert_element_type x1, other arithmetic, local(): return (dq.astype(BF16), dk.astype(BF16), dv.astype(BF16))  22.9 us
    dot_general x9, matrix products, _pair(): s = jnp.einsum('bqhd,bkhd->bhqk', q, k, preferred_element_type=F32) * scale  22.4 us
  transfers between devices with their start and end apart: 36, of which 14 were waited for; matrix products, arithmetic and copies ran while one was open for 17% of the time, Pallas kernels for 0%

commit v1 on v0

v1 whole, which is shorter than its diff:
```python
import functools

import jax
import jax.numpy as jnp
from jax import lax
from jax.experimental import pallas as pl
from jax.experimental.pallas import tpu as pltpu
from jax.sharding import PartitionSpec as P

F32 = jnp.float32
BF16 = jnp.bfloat16
MESH = pl.DeviceIdType.MESH
LOG2E = 1.4426950408889634

N = 8
SEG = 128
NSEG = 16
BLK = 512
FLIPS = ((0, 1, 0), (1, 0, 0), (1, 1, 0), (0, 1, 1), (1, 0, 1), (1, 1, 1), (0, 0, 1))


def _flip(d, flips):
    fy, fx, fc = flips
    if fy:
        d = (d + 4) % 8
    if fx:
        d = d + 2 - 4 * ((d // 2) % 2)
    if fc:
        d = d + 1 - 2 * (d % 2)
    return d


def _nt(a, b):
    return lax.dot_general(a, b, (((1,), (1,)), ((), ())), preferred_element_type=F32)


def _tn(a, b):
    return lax.dot_general(a, b, (((0,), (0,)), ((), ())), preferred_element_type=F32)


def _nn(a, b):
    return lax.dot_general(a, b, (((1,), (0,)), ((), ())), preferred_element_type=F32)


def _kernel(hl, scale, q, k, v, do, ld, dq, dk, dv, xin, ldin, obuf, dqacc, dkacc, dvacc,
            send_in, recv_in, send_ld, recv_ld, send_out, recv_out):
    me = lax.axis_index('cp')
    peers = [_flip(me, f) for f in FLIPS]

    barrier = pltpu.get_barrier_semaphore()
    for p in peers:
        pl.semaphore_signal(barrier, inc=1, device_id={'cp': p}, device_id_type=MESH)
    pl.semaphore_wait(barrier, N - 1)

    lo = pl.ds(pl.multiple_of(me * SEG, SEG), SEG)
    hi = pl.ds(pl.multiple_of((NSEG - 1 - me) * SEG, SEG), SEG)

    for half, seg in ((0, me), (1, NSEG - 1 - me)):
        for n, p in enumerate(peers):
            pltpu.make_async_remote_copy(ld.at[p, half], ldin.at[seg], send_ld, recv_ld,
                                         device_id={'cp': p}, device_id_type=MESH).start()
        pltpu.make_async_copy(ld.at[me, half], ldin.at[seg], recv_ld).start()

    for h in range(hl):
        for t, x in enumerate((q, k, v, do)):
            for half, rows in ((0, lo), (1, hi)):
                src = x.at[me * hl + h, pl.ds(half * SEG, SEG)]
                pltpu.make_async_copy(src, xin.at[h, t, rows], recv_in.at[h]).start()
        for p in peers:
            for t, x in enumerate((q, k, v, do)):
                for half, rows in ((0, lo), (1, hi)):
                    src = x.at[p * hl + h, pl.ds(half * SEG, SEG)]
                    pltpu.make_async_remote_copy(src, xin.at[h, t, rows], send_in, recv_in.at[h],
                                                 device_id={'cp': p}, device_id_type=MESH).start()

    pltpu.make_async_copy(ldin, ldin, recv_ld).wait()

    nblk = NSEG * SEG // BLK
    per = BLK // SEG

    def head(h, carry):
        pltpu.make_async_copy(xin.at[h], xin.at[h], recv_in.at[h]).wait()
        dqacc[...] = jnp.zeros_like(dqacc)

        for j in range(nblk):
            kr = pl.ds(j * BLK, BLK)

            def tile(i, masked):
                qr = pl.ds(pl.multiple_of(i * BLK, BLK), BLK)
                qb, dob = xin[h, 0, qr, :], xin[h, 3, qr, :]
                kb, vb = xin[h, 1, kr, :], xin[h, 2, kr, :]
                l2 = jnp.concatenate([ldin[i * per + s, pl.ds(2 * h, 1), :] for s in range(per)], axis=1)
                dl = jnp.concatenate([ldin[i * per + s, pl.ds(2 * h + 1, 1), :] for s in range(per)], axis=1)
                p = jnp.exp2(_nt(kb, qb) * (scale * LOG2E) - l2)
                if masked:
                    key = lax.broadcasted_iota(jnp.int32, (BLK, BLK), 0)
                    query = lax.broadcasted_iota(jnp.int32, (BLK, BLK), 1)
                    p = jnp.where(key <= query, p, 0.0)
                ds = (p * (_nt(vb, dob) - dl)).astype(BF16)
                dvb = _nn(p.astype(BF16), dob)
                dkb = _nn(ds, qb)
                dqacc[qr, :] += _tn(ds, kb)
                return dkb, dvb

            dkb, dvb = tile(j, True)
            dkacc[...] = dkb
            dvacc[...] = dvb

            @pl.loop(j + 1, nblk)
            def _(i):
                dkb, dvb = tile(i, False)
                dkacc[...] += dkb
                dvacc[...] += dvb

            obuf[h, 1, kr, :] = (dkacc[...] * scale).astype(BF16)
            obuf[h, 2, kr, :] = dvacc[...].astype(BF16)
        obuf[h, 0] = (dqacc[...] * scale).astype(BF16)

        mine = me * hl + h
        for p in peers:
            for t, x in enumerate((dq, dk, dv)):
                for half, seg in ((0, p), (1, NSEG - 1 - p)):
                    src = obuf.at[h, t, pl.ds(pl.multiple_of(seg * SEG, SEG), SEG)]
                    pltpu.make_async_remote_copy(src, x.at[mine, pl.ds(half * SEG, SEG)], send_out, recv_out.at[t],
                                                 device_id={'cp': p}, device_id_type=MESH).start()
        for t, x in enumerate((dq, dk, dv)):
            for half, rows in ((0, lo), (1, hi)):
                pltpu.make_async_copy(obuf.at[h, t, rows], x.at[mine, pl.ds(half * SEG, SEG)], recv_out.at[t]).start()
        return carry

    lax.fori_loop(0, hl, head, 0)

    far = pl.ds(0, (N - 1) * NSEG * SEG // N)
    pltpu.make_async_copy(ldin.at[pl.ds(0, 2 * (N - 1))], ldin.at[pl.ds(0, 2 * (N - 1))], send_ld).wait()
    pltpu.make_async_copy(xin.at[:, :, far], xin.at[:, :, far], send_in).wait()
    pltpu.make_async_copy(obuf.at[:, :, far], obuf.at[:, :, far], send_out).wait()
    for t, x in enumerate((dq, dk, dv)):
        pltpu.make_async_copy(x, x, recv_out.at[t]).wait()


def solution(mesh):
    spec = P('data', 'cp', None, None)
    lspec = P('data', None, 'cp')

    def local(q, k, v, o, lse, do):
        b, tok, heads, dim = q.shape
        hl = heads // N
        delta = jnp.einsum('bqhd,bqhd->bhq', do, o, preferred_element_type=F32)[0]
        ld = jnp.stack([lse[0] * LOG2E, delta], axis=1).reshape(N, 2 * hl, 2, SEG).transpose(0, 2, 1, 3)
        qt, kt, vt, dot = (jnp.swapaxes(x[0], 0, 1) for x in (q, k, v, do))
        any_ = pl.BlockSpec(memory_space=pl.ANY)
        seq = NSEG * SEG
        outs = pl.pallas_call(
            functools.partial(_kernel, hl, dim ** -0.5),
            out_shape=[jax.ShapeDtypeStruct((heads, tok, dim), BF16)] * 3,
            in_specs=[any_] * 5,
            out_specs=[any_] * 3,
            scratch_shapes=[
                pltpu.VMEM((hl, 4, seq, dim), BF16),
                pltpu.VMEM((NSEG, 2 * hl, SEG), F32),
                pltpu.VMEM((hl, 3, seq, dim), BF16),
                pltpu.VMEM((seq, dim), F32),
                pltpu.VMEM((BLK, dim), F32),
                pltpu.VMEM((BLK, dim), F32),
                pltpu.SemaphoreType.DMA,
                pltpu.SemaphoreType.DMA((hl,)),
                pltpu.SemaphoreType.DMA,
                pltpu.SemaphoreType.DMA,
                pltpu.SemaphoreType.DMA,
                pltpu.SemaphoreType.DMA((3,)),
            ],
            compiler_params=pltpu.CompilerParams(collective_id=0, has_side_effects=True,
                                                 vmem_limit_bytes=56 * 2 ** 20),
            name='attention_backward',
        )(qt, kt, vt, dot, ld)
        return tuple(jnp.swapaxes(x, 0, 1)[None] for x in outs)

    return jax.shard_map(local, mesh=mesh, in_specs=(spec, spec, spec, spec, lspec, spec),
                         out_specs=(spec, spec, spec), check_vma=False)
```

time: 916 us -> 190 us (0.21)
  the two profiles are of different devices: /device:TPU:0 before, /device:TPU:1 now
where the time goes in v1:
time: 190 us
  Pallas kernels  163 us (86%)
  local copies, waits for them, and re-layouts  19.6 us (10%)
  other arithmetic  6.26 us (3%)
    pallas_call x1, Pallas kernels, local(): pl.pallas_call(functools.partial(_kernel, hl, dim ** (-0.5)), out_shape=[...  163 us
    unnamed x15, local copies, waits for them, and re-layouts  9.78 us
    transpose x2, local copies, waits for them, and re-layouts, local(): qt, kt, vt, dot = (jnp.swapaxes(x[0], 0, 1) for x in (q, k, v, do))  9.03 us
    unnamed x2, other arithmetic  5.48 us

profile of v1, /device:TPU:1, one launch (start us, length us, event | category | flops | bytes accessed | tf_op | source)
XLA Modules:
  0.0 189.9 jit_solution(12604730759521069324)
XLA Ops:
  0.6 0.8 multiply_bitcast_fusion
  1.4 0.0 copy-start.1
  1.4 2.4 %copy_convert_fusion = f32[32,256,128]{2,1,0:T(8,128)S(1)} fusion(bf16[32,256,128]{2,0,1:T(8,128)(2,1)} %bitcast.38), kind=kLoop, calls=%fused_computation.1 | loop fusion | flops 1048576 | bytes 6291456
  3.8 0.0 copy-done.1
  3.8 0.0 copy-start.4
  3.8 3.1 %multiply_reduce_fusion = f32[32,256]{0,1:T(8,128)S(1)} fusion(f32[32,256,128]{2,1,0:T(8,128)S(1)} %copy_convert_fusion, bf16[1,256,32,128]{3,2,1,0:T(8,128)(2,1)S(1)} %copy-done.1), kind=kLoop, calls=%fused_computation | loop fusion | flops 3137536 | bytes 6324224
  6.9 0.1 copy.31
  7.0 0.1 copy.20
  7.1 0.1 reshape.28
  7.1 0.6 copy.40
  7.8 0.0 copy-done.4
  7.8 0.0 copy-start
  7.8 0.0 copy-start.5
  7.8 5.4 %copy_bitcast_fusion.2 = (bf16[32,256,128]{2,1,0:T(8,128)(2,1)}, bf16[32,256,128]{2,1,0:T(8,128)(2,1)}) fusion(bf16[1,256,32,128]{3,2,1,0:T(8,128)(2,1)S(1)} %copy-done.4, bf16[1,256,32,128]{3,2,1,0:T(8,128)(2,1)} %param.6), kind=kLoop, calls=%fused_computation.4 | loop fusion | bytes 8388608 | tf_op jit(solution)/shard_map/transpose | solution.py:150
  13.1 0.0 copy-done
  13.2 0.0 copy-done.5
  13.2 3.7 %copy_bitcast_fusion = (bf16[32,256,128]{2,1,0:T(8,128)(2,1)}, bf16[32,256,128]{2,1,0:T(8,128)(2,1)}) fusion(bf16[1,256,32,128]{3,2,1,0:T(8,128)(2,1)S(1)} %copy-done, bf16[1,256,32,128]{3,2,1,0:T(8,128)(2,1)S(1)} %copy-done.5), kind=kLoop, calls=%fused_computation.2 | loop fusion | bytes 8388608 | tf_op jit(solution)/shard_map/transpose | solution.py:150
  16.8 163.3 %attention_backward.1 = (bf16[32,256,128]{2,1,0:T(8,128)(2,1)}, bf16[32,256,128]{2,1,0:T(8,128)(2,1)}, bf16[32,256,128]{2,1,0:T(8,128)(2,1)}) custom-call(bf16[32,256,128]{2,1,0:T(8,128)(2,1)} %get-tuple-element.18.q, bf16[32,256,128]{2,1,0:T(8,128)(2,1)} %get-tuple-element.17.k, bf16[32,256,128]{2,1,0:T(8,128)(2,1)} %get-tuple-element.16.v, ...), custom_call_target="tpu_custom_call" | custom-call | tf_op jit(solution)/shard_map/attention_backward/pallas_call | solution.py:153
  180.1 0.0 copy-start.3
  180.1 4.4 %copy.22 = bf16[1,256,32,128]{3,2,1,0:T(8,128)(2,1)} copy(bf16[1,256,32,128]{3,1,2,0:T(8,128)(2,1)} %bitcast.41) | data formatting | bytes 4194304
  184.5 0.0 copy-done.3
  184.5 0.0 copy-start.2
  184.6 2.7 %copy.23 = bf16[1,256,32,128]{3,2,1,0:T(8,128)(2,1)} copy(bf16[1,256,32,128]{3,1,2,0:T(8,128)(2,1)S(1)} %bitcast.40) | data formatting | bytes 4194304
  187.2 0.0 copy-done.2
  187.2 2.7 %copy.24 = bf16[1,256,32,128]{3,2,1,0:T(8,128)(2,1)} copy(bf16[1,256,32,128]{3,1,2,0:T(8,128)(2,1)S(1)} %bitcast.39) | data formatting | bytes 4194304
  (1 shorter events, 0.0 us)
Async XLA Ops:
  1.4 2.4 %copy-start.1 = (bf16[1,256,32,128]{3,2,1,0:T(8,128)(2,1)S(1)}, bf16[1,256,32,128]{3,2,1,0:T(8,128)(2,1)}, u32[]{:S(2)}) copy-start(bf16[1,256,32,128]{3,2,1,0:T(8,128)(2,1)} %param.9) | copy-start | bytes 6291460
  3.8 4.0 %copy-start.4 = (bf16[1,256,32,128]{3,2,1,0:T(8,128)(2,1)S(1)}, bf16[1,256,32,128]{3,2,1,0:T(8,128)(2,1)}, u32[]{:S(2)}) copy-start(bf16[1,256,32,128]{3,2,1,0:T(8,128)(2,1)} %param.7) | copy-start | bytes 6291460
  7.8 5.4 %copy-start = (bf16[1,256,32,128]{3,2,1,0:T(8,128)(2,1)S(1)}, bf16[1,256,32,128]{3,2,1,0:T(8,128)(2,1)}, u32[]{:S(2)}) copy-start(bf16[1,256,32,128]{3,2,1,0:T(8,128)(2,1)} %param.11) | copy-start | bytes 6291460
  7.8 5.4 %copy-start.5 = (bf16[1,256,32,128]{3,2,1,0:T(8,128)(2,1)S(1)}, bf16[1,256,32,128]{3,2,1,0:T(8,128)(2,1)}, u32[]{:S(2)}) copy-start(bf16[1,256,32,128]{3,2,1,0:T(8,128)(2,1)} %param.8) | copy-start | bytes 6291460
  180.1 4.4 %copy-start.3 = (bf16[32,256,128]{2,1,0:T(8,128)(2,1)S(1)}, bf16[32,256,128]{2,1,0:T(8,128)(2,1)}, u32[]{:S(2)}) copy-start(bf16[32,256,128]{2,1,0:T(8,128)(2,1)} %get-tuple-element.7) | copy-start | bytes 6291460
  184.5 2.7 %copy-start.2 = (bf16[32,256,128]{2,1,0:T(8,128)(2,1)S(1)}, bf16[32,256,128]{2,1,0:T(8,128)(2,1)}, u32[]{:S(2)}) copy-start(bf16[32,256,128]{2,1,0:T(8,128)(2,1)} %get-tuple-element.8) | copy-start | bytes 6291460

commit v2 on v1

v2 whole, which is shorter than its diff:
```python
import functools

import jax
import jax.numpy as jnp
from jax import lax
from jax.experimental import pallas as pl
from jax.experimental.pallas import tpu as pltpu
from jax.sharding import PartitionSpec as P

F32 = jnp.float32
BF16 = jnp.bfloat16
MESH = pl.DeviceIdType.MESH
LOG2E = 1.4426950408889634

N = 8
SEG = 128
NSEG = 16
BLK = 512
CHIPS = ((0, 1), (1, 0), (1, 1), (0, 0))
CHUNK = 64


def _chip(c, flips):
    fy, fx = flips
    if fy:
        c = (c + 2) % 4
    if fx:
        c = c + 1 - 2 * (c % 2)
    return c


def _nt(a, b):
    return lax.dot_general(a, b, (((1,), (1,)), ((), ())), preferred_element_type=F32)


def _tn(a, b):
    return lax.dot_general(a, b, (((0,), (0,)), ((), ())), preferred_element_type=F32)


def _nn(a, b):
    return lax.dot_general(a, b, (((1,), (0,)), ((), ())), preferred_element_type=F32)


def _swap(dst, src, tok, inverse=False):
    @pl.loop(0, tok // CHUNK)
    def _(i):
        r = pl.ds(pl.multiple_of(i * CHUNK, CHUNK), CHUNK)
        if inverse:
            dst[r] = jnp.swapaxes(src[:, r, :], 0, 1)
        else:
            dst[:, r, :] = jnp.swapaxes(src[r], 0, 1)


def _kernel(hl, scale, q, k, v, do, o, lse, dq, dk, dv, nat, onat, lsev, hm, ohm, ldst, xin, ldin, obuf, rin,
            dqacc, dkacc, dvacc, nat_sem, lse_sem, send_in, recv_in, send_ld, recv_ld, send_out, recv_out):
    me = lax.axis_index('cp')
    core = me % 2
    chips = [_chip(me // 2, f) for f in CHIPS]
    tok = nat.shape[2]
    peers = [[2 * chip + b for b in (0, 1)] for chip in chips]
    other = me + 1 - 2 * core
    remote = [p for ps in peers[:3] for p in ps] + [other]

    barrier = pltpu.get_barrier_semaphore()
    for p in remote:
        pl.semaphore_signal(barrier, inc=1, device_id={'cp': p}, device_id_type=MESH)

    inputs = (q, k, v, do)
    group = [pl.ds(pl.multiple_of(chip * 2 * hl, 2 * hl), 2 * hl) for chip in chips]

    def load(t, c):
        return pltpu.make_async_copy(inputs[t].at[:, group[c]], nat.at[t, c], nat_sem.at[t, c])

    def load_o(c):
        return pltpu.make_async_copy(o.at[:, group[c]], onat.at[c], nat_sem.at[4, c])

    for t in range(4):
        for c in range(4):
            load(t, c).start()
    for c in range(4):
        load_o(c).start()
    load_lse = pltpu.make_async_copy(lse, lsev, lse_sem)
    load_lse.start()

    segs = (me, NSEG - 1 - me)
    rows = [pl.ds(pl.multiple_of(s * SEG, SEG), SEG) for s in segs]
    halves = [pl.ds(half * SEG, SEG) for half in (0, 1)]

    def send(t, c, h):
        for half in (0, 1):
            dst = xin.at[h, t, rows[half]]
            if c < 3:
                for b in (0, 1):
                    pltpu.make_async_remote_copy(hm.at[t, c, b * hl + h, halves[half]], dst, send_in, recv_in.at[h],
                                                 device_id={'cp': peers[c][b]}, device_id_type=MESH).start()
            else:
                pltpu.make_async_remote_copy(hm.at[t, c, (1 - core) * hl + h, halves[half]], dst, send_in, recv_in.at[h],
                                             device_id={'cp': other}, device_id_type=MESH).start()
                pltpu.make_async_copy(hm.at[t, c, core * hl + h, halves[half]], dst, recv_in.at[h]).start()

    units = [(t, c) for t in range(4) for c in range(4)]
    for n, (t, c) in enumerate(units):
        load(t, c).wait()
        _swap(hm.at[t, c], nat.at[t, c], tok)
        if n == 0:
            pl.semaphore_wait(barrier, N - 1)
        else:
            send(*units[n - 1], 0)

    row = lax.broadcasted_iota(jnp.int32, (2 * hl, nat.shape[-1]), 0)
    load_lse.wait()
    for c in range(4):
        load_o(c).wait()
        _swap(ohm, onat.at[c], tok)
        if c == 0:
            send(*units[-1], 0)
        delta = jnp.zeros((2 * hl, tok), F32)
        for g in range(2 * hl):
            prod = hm[3, c, g].astype(F32) * ohm[g].astype(F32)
            top = prod.astype(BF16)
            low = (prod - top.astype(F32)).astype(BF16)
            pick = jnp.where(row == g, 1.0, 0.0).astype(BF16)
            delta = delta + (_nt(pick, top) + _nt(pick, low))
        l2 = lsev[group[c], :] * LOG2E
        for b in (0, 1):
            for half in (0, 1):
                ldst[c, b, half, 0:hl, :] = l2[b * hl:(b + 1) * hl, half * SEG:(half + 1) * SEG]
                ldst[c, b, half, hl:2 * hl, :] = delta[b * hl:(b + 1) * hl, half * SEG:(half + 1) * SEG]
    for half in (0, 1):
        dst = ldin.at[segs[half]]
        for c in range(3):
            for b in (0, 1):
                pltpu.make_async_remote_copy(ldst.at[c, b, half], dst, send_ld, recv_ld,
                                             device_id={'cp': peers[c][b]}, device_id_type=MESH).start()
        pltpu.make_async_remote_copy(ldst.at[3, 1 - core, half], dst, send_ld, recv_ld,
                                     device_id={'cp': other}, device_id_type=MESH).start()
        pltpu.make_async_copy(ldst.at[3, core, half], dst, recv_ld).start()
    for h in range(1, hl):
        for c in range(4):
            for t in range(4):
                send(t, c, h)

    pltpu.make_async_copy(ldin, ldin, recv_ld).wait()

    nblk = NSEG * SEG // BLK
    per = BLK // SEG

    def head(h, carry):
        pltpu.make_async_copy(xin.at[h], xin.at[h], recv_in.at[h]).wait()
        dqacc[...] = jnp.zeros_like(dqacc)

        for j in range(nblk):
            kr = pl.ds(j * BLK, BLK)

            def tile(i, masked):
                qr = pl.ds(pl.multiple_of(i * BLK, BLK), BLK)
                qb, dob = xin[h, 0, qr, :], xin[h, 3, qr, :]
                kb, vb = xin[h, 1, kr, :], xin[h, 2, kr, :]
                l2 = jnp.concatenate([ldin[i * per + s, pl.ds(h, 1), :] for s in range(per)], axis=1)
                dl = jnp.concatenate([ldin[i * per + s, pl.ds(hl + h, 1), :] for s in range(per)], axis=1)
                p = jnp.exp2(_nt(kb, qb) * (scale * LOG2E) - l2)
                if masked:
                    key = lax.broadcasted_iota(jnp.int32, (BLK, BLK), 0)
                    query = lax.broadcasted_iota(jnp.int32, (BLK, BLK), 1)
                    p = jnp.where(key <= query, p, 0.0)
                ds = (p * (_nt(vb, dob) - dl)).astype(BF16)
                dvb = _nn(p.astype(BF16), dob)
                dkb = _nn(ds, qb)
                dqacc[qr, :] += _tn(ds, kb)
                return dkb, dvb

            dkb, dvb = tile(j, True)
            dkacc[...] = dkb
            dvacc[...] = dvb

            @pl.loop(j + 1, nblk)
            def _(i):
                dkb, dvb = tile(i, False)
                dkacc[...] += dkb
                dvacc[...] += dvb

            obuf[h, 1, kr, :] = (dkacc[...] * scale).astype(BF16)
            obuf[h, 2, kr, :] = dvacc[...].astype(BF16)
        obuf[h, 0] = (dqacc[...] * scale).astype(BF16)

        mine = me * hl + h
        for t in (1, 2, 0):
            for p in remote:
                for half, seg in ((0, p), (1, NSEG - 1 - p)):
                    src = obuf.at[h, t, pl.ds(pl.multiple_of(seg * SEG, SEG), SEG)]
                    pltpu.make_async_remote_copy(src, rin.at[t, mine, halves[half]], send_out, recv_out.at[t],
                                                 device_id={'cp': p}, device_id_type=MESH).start()
            for half in (0, 1):
                pltpu.make_async_copy(obuf.at[h, t, rows[half]], rin.at[t, mine, halves[half]], recv_out.at[t]).start()
        return carry

    lax.fori_loop(0, hl, head, 0)

    for t, x in ((1, dk), (2, dv), (0, dq)):
        pltpu.make_async_copy(rin.at[t], rin.at[t], recv_out.at[t]).wait()
        for g in range(N // 2):
            heads = pl.ds(g * 2 * hl, 2 * hl)
            _swap(x.at[:, heads], rin.at[t, heads], tok, inverse=True)
    far = pl.ds(0, (N - 1) * NSEG * SEG // N)
    pltpu.make_async_copy(ldin.at[pl.ds(0, 2 * (N - 1))], ldin.at[pl.ds(0, 2 * (N - 1))], send_ld).wait()
    pltpu.make_async_copy(xin.at[:, :, far], xin.at[:, :, far], send_in).wait()
    pltpu.make_async_copy(obuf.at[:, :, far], obuf.at[:, :, far], send_out).wait()


def solution(mesh):
    spec = P('data', 'cp', None, None)
    lspec = P('data', None, 'cp')

    def local(q, k, v, o, lse, do):
        b, tok, heads, dim = q.shape
        hl = heads // N
        any_ = pl.BlockSpec(memory_space=pltpu.HBM)
        seq = NSEG * SEG
        outs = pl.pallas_call(
            functools.partial(_kernel, hl, dim ** -0.5),
            out_shape=[jax.ShapeDtypeStruct((tok, heads, dim), BF16)] * 3,
            in_specs=[any_] * 6,
            out_specs=[pl.BlockSpec(memory_space=pltpu.VMEM)] * 3,
            scratch_shapes=[
                pltpu.VMEM((4, N // 2, tok, 2 * hl, dim), BF16),
                pltpu.VMEM((N // 2, tok, 2 * hl, dim), BF16),
                pltpu.VMEM((heads, tok), F32),
                pltpu.VMEM((4, N // 2, 2 * hl, tok, dim), BF16),
                pltpu.VMEM((2 * hl, tok, dim), BF16),
                pltpu.VMEM((N // 2, 2, 2, 2 * hl, SEG), F32),
                pltpu.VMEM((hl, 4, seq, dim), BF16),
                pltpu.VMEM((NSEG, 2 * hl, SEG), F32),
                pltpu.VMEM((hl, 3, seq, dim), BF16),
                pltpu.VMEM((3, heads, tok, dim), BF16),
                pltpu.VMEM((seq, dim), F32),
                pltpu.VMEM((BLK, dim), F32),
                pltpu.VMEM((BLK, dim), F32),
                pltpu.SemaphoreType.DMA((5, N // 2)),
                pltpu.SemaphoreType.DMA,
                pltpu.SemaphoreType.DMA,
                pltpu.SemaphoreType.DMA((hl,)),
                pltpu.SemaphoreType.DMA,
                pltpu.SemaphoreType.DMA,
                pltpu.SemaphoreType.DMA,
                pltpu.SemaphoreType.DMA((3,)),
            ],
            compiler_params=pltpu.CompilerParams(collective_id=0, has_side_effects=True,
                                                 vmem_limit_bytes=47 * 2 ** 20),
            name='attention_backward',
        )(q[0], k[0], v[0], do[0], o[0], lse[0])
        return tuple(x[None] for x in outs)

    return jax.shard_map(local, mesh=mesh, in_specs=(spec, spec, spec, spec, lspec, spec),
                         out_specs=(spec, spec, spec), check_vma=False)
```

time: 190 us -> 170 us (0.89)
  local copies, waits for them, and re-layouts: 19.6 us -> 4.71 us
  other arithmetic: 6.26 us -> 0 us
  Pallas kernels: 163 us -> 165 us
    transpose x2 -> x0, local copies, waits for them, and re-layouts: 9.03 us -> none  [local(): qt, kt, vt, dot = (jnp.swapaxes(x[0], 0, 1) for x in (q, k, v, do))]
    unnamed x2 -> x0, other arithmetic: 5.48 us -> none
    unnamed x15 -> x5, local copies, waits for them, and re-layouts: 9.78 us -> 4.71 us
where the time goes in v2:
time: 170 us
  Pallas kernels  165 us (97%)
  local copies, waits for them, and re-layouts  4.71 us (3%)
    pallas_call x1, Pallas kernels, local(): pl.pallas_call(functools.partial(_kernel, hl, dim ** (-0.5)), out_shape=[...  165 us
    unnamed x5, local copies, waits for them, and re-layouts  4.71 us

profile of v2, /device:TPU:1, one launch (start us, length us, event | category | flops | bytes accessed | tf_op | source)
XLA Modules:
  0.0 170.1 jit_solution(11457736089202516856)
XLA Ops:
  0.6 0.0 copy-start
  0.6 0.7 copy-done
  1.4 164.7 %attention_backward.1 = (bf16[256,32,128]{2,1,0:T(8,128)(2,1)S(1)}, bf16[256,32,128]{2,1,0:T(8,128)(2,1)S(1)}, bf16[256,32,128]{2,1,0:T(8,128)(2,1)S(1)}) custom-call(bf16[256,32,128]{2,1,0:T(8,128)(2,1)} %bitcast.13, bf16[256,32,128]{2,1,0:T(8,128)(2,1)} %bitcast.14, bf16[256,32,128]{2,1,0:T(8,128)(2,1)} %bitcast.15, bf16[256,32,128]{2,1,0:T(8,128)(2,1)} %bitcast.16, ...), custom_call_target="tpu_custom_call" | custom-call | tf_op jit(solution)/shard_map/attention_backward/pallas_call | solution.py:219
  166.1 1.3 copy.12
  167.5 1.3 copy.13
  168.8 1.3 copy.14
Async XLA Ops:
  0.6 0.8 copy-start

commit v3 on v2

--- a/solution.py
+++ b/solution.py
@@ -18,6 +18,7 @@
 BLK = 512
 CHIPS = ((0, 1), (1, 0), (1, 1), (0, 0))
 CHUNK = 64
+AHEAD = 4
 
 
 def _chip(c, flips):
@@ -51,7 +52,7 @@
             dst[:, r, :] = jnp.swapaxes(src[r], 0, 1)
 
 
-def _kernel(hl, scale, q, k, v, do, o, lse, dq, dk, dv, nat, onat, lsev, hm, ohm, ldst, xin, ldin, obuf, rin,
+def _kernel(hl, scale, q, k, v, do, o, lse, dqh, dk, dv, nat, onat, lsev, hm, ohm, ldst, xin, ldin, obuf, rin,
             dqacc, dkacc, dvacc, nat_sem, lse_sem, send_in, recv_in, send_ld, recv_ld, send_out, recv_out):
     me = lax.axis_index('cp')
     core = me % 2
@@ -74,11 +75,10 @@
     def load_o(c):
         return pltpu.make_async_copy(o.at[:, group[c]], onat.at[c], nat_sem.at[4, c])
 
-    for t in range(4):
-        for c in range(4):
-            load(t, c).start()
-    for c in range(4):
-        load_o(c).start()
+    units = [(t, c) for t in range(4) for c in range(4)]
+    loads = [load(*u) for u in units] + [load_o(c) for c in range(4)]
+    for copy in loads[:AHEAD]:
+        copy.start()
     load_lse = pltpu.make_async_copy(lse, lsev, lse_sem)
     load_lse.start()
 
@@ -98,9 +98,10 @@
                                              device_id={'cp': other}, device_id_type=MESH).start()
                 pltpu.make_async_copy(hm.at[t, c, core * hl + h, halves[half]], dst, recv_in.at[h]).start()
 
-    units = [(t, c) for t in range(4) for c in range(4)]
     for n, (t, c) in enumerate(units):
-        load(t, c).wait()
+        if n + AHEAD < len(loads):
+            loads[n + AHEAD].start()
+        loads[n].wait()
         _swap(hm.at[t, c], nat.at[t, c], tok)
         if n == 0:
             pl.semaphore_wait(barrier, N - 1)
@@ -110,7 +111,7 @@
     row = lax.broadcasted_iota(jnp.int32, (2 * hl, nat.shape[-1]), 0)
     load_lse.wait()
     for c in range(4):
-        load_o(c).wait()
+        loads[16 + c].wait()
         _swap(ohm, onat.at[c], tok)
         if c == 0:
             send(*units[-1], 0)
@@ -184,29 +185,45 @@
         obuf[h, 0] = (dqacc[...] * scale).astype(BF16)
 
         mine = me * hl + h
-        for t in (1, 2, 0):
+        for t, x in ((1, rin.at[0]), (2, rin.at[1]), (0, dqh)):
             for p in remote:
                 for half, seg in ((0, p), (1, NSEG - 1 - p)):
                     src = obuf.at[h, t, pl.ds(pl.multiple_of(seg * SEG, SEG), SEG)]
-                    pltpu.make_async_remote_copy(src, rin.at[t, mine, halves[half]], send_out, recv_out.at[t],
+                    pltpu.make_async_remote_copy(src, x.at[mine, halves[half]], send_out, recv_out.at[t],
                                                  device_id={'cp': p}, device_id_type=MESH).start()
             for half in (0, 1):
-                pltpu.make_async_copy(obuf.at[h, t, rows[half]], rin.at[t, mine, halves[half]], recv_out.at[t]).start()
+                pltpu.make_async_copy(obuf.at[h, t, rows[half]], x.at[mine, halves[half]], recv_out.at[t]).start()
         return carry
 
     lax.fori_loop(0, hl, head, 0)
 
-    for t, x in ((1, dk), (2, dv), (0, dq)):
-        pltpu.make_async_copy(rin.at[t], rin.at[t], recv_out.at[t]).wait()
+    for t, x in ((1, dk), (2, dv)):
+        src = rin.at[t - 1]
+        pltpu.make_async_copy(src, src, recv_out.at[t]).wait()
         for g in range(N // 2):
             heads = pl.ds(g * 2 * hl, 2 * hl)
-            _swap(x.at[:, heads], rin.at[t, heads], tok, inverse=True)
+            _swap(x.at[:, heads], src.at[heads], tok, inverse=True)
+    pltpu.make_async_copy(dqh, dqh, recv_out.at[0]).wait()
     far = pl.ds(0, (N - 1) * NSEG * SEG // N)
     pltpu.make_async_copy(ldin.at[pl.ds(0, 2 * (N - 1))], ldin.at[pl.ds(0, 2 * (N - 1))], send_ld).wait()
     pltpu.make_async_copy(xin.at[:, :, far], xin.at[:, :, far], send_in).wait()
     pltpu.make_async_copy(obuf.at[:, :, far], obuf.at[:, :, far], send_out).wait()
 
 
+def _close(dqh, dkt, dvt, dq, dk, dv, dqt, sem):
+    copies = [pltpu.make_async_copy(dkt, dk, sem.at[0]), pltpu.make_async_copy(dvt, dv, sem.at[1])]
+    for copy in copies:
+        copy.start()
+    heads, tok = dqh.shape[:2]
+    for g in range(heads // 8):
+        part = pl.ds(g * 8, 8)
+        _swap(dqt.at[g], dqh.at[part], tok, inverse=True)
+        copies.append(pltpu.make_async_copy(dqt.at[g], dq.at[:, part], sem.at[2 + g]))
+        copies[-1].start()
+    for copy in copies:
+        copy.wait()
+
+
 def solution(mesh):
     spec = P('data', 'cp', None, None)
     lspec = P('data', None, 'cp')
@@ -215,12 +232,13 @@
         b, tok, heads, dim = q.shape
         hl = heads // N
         any_ = pl.BlockSpec(memory_space=pltpu.HBM)
+        vmem = pl.BlockSpec(memory_space=pltpu.VMEM)
         seq = NSEG * SEG
         outs = pl.pallas_call(
             functools.partial(_kernel, hl, dim ** -0.5),
-            out_shape=[jax.ShapeDtypeStruct((tok, heads, dim), BF16)] * 3,
+            out_shape=[jax.ShapeDtypeStruct((heads, tok, dim), BF16)] + [jax.ShapeDtypeStruct((tok, heads, dim), BF16)] * 2,
             in_specs=[any_] * 6,
-            out_specs=[pl.BlockSpec(memory_space=pltpu.VMEM)] * 3,
+            out_specs=[vmem] * 3,
             scratch_shapes=[
                 pltpu.VMEM((4, N // 2, tok, 2 * hl, dim), BF16),
                 pltpu.VMEM((N // 2, tok, 2 * hl, dim), BF16),
@@ -231,7 +249,7 @@
                 pltpu.VMEM((hl, 4, seq, dim), BF16),
                 pltpu.VMEM((NSEG, 2 * hl, SEG), F32),
                 pltpu.VMEM((hl, 3, seq, dim), BF16),
-                pltpu.VMEM((3, heads, tok, dim), BF16),
+                pltpu.VMEM((2, heads, tok, dim), BF16),
                 pltpu.VMEM((seq, dim), F32),
                 pltpu.VMEM((BLK, dim), F32),
                 pltpu.VMEM((BLK, dim), F32),
@@ -245,10 +263,20 @@
                 pltpu.SemaphoreType.DMA((3,)),
             ],
             compiler_params=pltpu.CompilerParams(collective_id=0, has_side_effects=True,
-                                                 vmem_limit_bytes=47 * 2 ** 20),
+                                                 vmem_limit_bytes=46 * 2 ** 20),
             name='attention_backward',
         )(q[0], k[0], v[0], do[0], o[0], lse[0])
-        return tuple(x[None] for x in outs)
+        grads = pl.pallas_call(
+            _close,
+            out_shape=[jax.ShapeDtypeStruct((tok, heads, dim), BF16)] * 3,
+            in_specs=[vmem] * 3,
+            out_specs=[any_] * 3,
+            scratch_shapes=[pltpu.VMEM((heads // 8, tok, 8, dim), BF16),
+                            pltpu.SemaphoreType.DMA((2 + heads // 8,))],
+            compiler_params=pltpu.CompilerParams(vmem_limit_bytes=16 * 2 ** 20),
+            name='close',
+        )(*outs)
+        return tuple(x[None] for x in grads)
 
     return jax.shard_map(local, mesh=mesh, in_specs=(spec, spec, spec, spec, lspec, spec),
                          out_specs=(spec, spec, spec), check_vma=False)

time: 170 us -> 168 us (0.988)
  local copies, waits for them, and re-layouts: 4.71 us -> 0.75 us
  Pallas kernels: 165 us -> 167 us
    unnamed x5 -> x2, local copies, waits for them, and re-layouts: 4.71 us -> 0.75 us
    pallas_call x0 -> x1, Pallas kernels: none -> 2.7 us  [local(): pl.pallas_call(_close, out_shape=[jax.ShapeDtypeStruct((tok, heads, dim),...]
where the time goes in v3:
time: 168 us
  Pallas kernels  167 us (99%)
    pallas_call x1, Pallas kernels, local(): pl.pallas_call(functools.partial(_kernel, hl, dim ** (-0.5)), out_shape=[...  164 us

profile of v3, /device:TPU:1, one launch (start us, length us, event | category | flops | bytes accessed | tf_op | source)
XLA Modules:
  0.0 168.1 jit_solution(4592156376287060406)
XLA Ops:
  0.6 0.0 copy-start
  0.6 0.7 copy-done
  1.4 164.0 %attention_backward.1 = (bf16[32,256,128]{2,1,0:T(8,128)(2,1)S(1)}, bf16[256,32,128]{2,1,0:T(8,128)(2,1)S(1)}, bf16[256,32,128]{2,1,0:T(8,128)(2,1)S(1)}) custom-call(bf16[256,32,128]{2,1,0:T(8,128)(2,1)} %bitcast.10, bf16[256,32,128]{2,1,0:T(8,128)(2,1)} %bitcast.11, bf16[256,32,128]{2,1,0:T(8,128)(2,1)} %bitcast.12, bf16[256,32,128]{2,1,0:T(8,128)(2,1)} %bitcast.13, ...), custom_call_target="tpu_custom_call" | custom-call | tf_op jit(solution)/shard_map/attention_backward/pallas_call | solution.py:237
  165.4 2.7 %close.1 = (bf16[256,32,128]{2,1,0:T(8,128)(2,1)}, bf16[256,32,128]{2,1,0:T(8,128)(2,1)}, bf16[256,32,128]{2,1,0:T(8,128)(2,1)}) custom-call(bf16[32,256,128]{2,1,0:T(8,128)(2,1)S(1)} %get-tuple-element.9.dqh, bf16[256,32,128]{2,1,0:T(8,128)(2,1)S(1)} %get-tuple-element.10.dkt, bf16[256,32,128]{2,1,0:T(8,128)(2,1)S(1)} %get-tuple-element.11.dvt), custom_call_target="tpu_custom_call" | custom-call | tf_op jit(solution)/shard_map/close/pallas_call | solution.py:269
Async XLA Ops:
  0.6 0.8 copy-start

commit v4 on v3

--- a/solution.py
+++ b/solution.py
@@ -19,6 +19,7 @@
 CHIPS = ((0, 1), (1, 0), (1, 1), (0, 0))
 CHUNK = 64
 AHEAD = 4
+RING = 6
 
 
 def _chip(c, flips):
@@ -52,12 +53,17 @@
             dst[:, r, :] = jnp.swapaxes(src[r], 0, 1)
 
 
-def _kernel(hl, scale, q, k, v, do, o, lse, dqh, dk, dv, nat, onat, lsev, hm, ohm, ldst, xin, ldin, obuf, rin,
-            dqacc, dkacc, dvacc, nat_sem, lse_sem, send_in, recv_in, send_ld, recv_ld, send_out, recv_out):
+def _kernel(hl, scale, q, k, v, do, o, lse, dqh, dk, dv, nat, lsev, hm, ohm, ldst, xin, ldin, obuf, rin,
+            dqacc, dkacc, dvacc, rel, loc, locld, lkv, ldq, gdq, rdq, fdq,
+            nat_sem, lse_sem, send_in, recv_in, send_ld, recv_ld, send_out, recv_out,
+            rel_sem, fwd_sem, send_loc, recv_loc, gdq_sem, send_fdq, rdq_sem):
     me = lax.axis_index('cp')
     core = me % 2
-    chips = [_chip(me // 2, f) for f in CHIPS]
-    tok = nat.shape[2]
+    chip = me // 2
+    chips = [_chip(chip, f) for f in CHIPS]
+    tok = nat.shape[1]
+    outer = chip != 0
+    last = pl.ds((NSEG - 2) * SEG, 2 * SEG)
     peers = [[2 * chip + b for b in (0, 1)] for chip in chips]
     other = me + 1 - 2 * core
     remote = [p for ps in peers[:3] for p in ps] + [other]
@@ -69,14 +75,9 @@
     inputs = (q, k, v, do)
     group = [pl.ds(pl.multiple_of(chip * 2 * hl, 2 * hl), 2 * hl) for chip in chips]
 
-    def load(t, c):
-        return pltpu.make_async_copy(inputs[t].at[:, group[c]], nat.at[t, c], nat_sem.at[t, c])
-
-    def load_o(c):
-        return pltpu.make_async_copy(o.at[:, group[c]], onat.at[c], nat_sem.at[4, c])
-
     units = [(t, c) for t in range(4) for c in range(4)]
-    loads = [load(*u) for u in units] + [load_o(c) for c in range(4)]
+    loads = [pltpu.make_async_copy(x.at[:, group[c]], nat.at[(4 * t + c) % RING], nat_sem.at[(4 * t + c) % RING])
+             for t, x in enumerate((*inputs, o)) for c in range(4)]
     for copy in loads[:AHEAD]:
         copy.start()
     load_lse = pltpu.make_async_copy(lse, lsev, lse_sem)
@@ -90,19 +91,44 @@
         for half in (0, 1):
             dst = xin.at[h, t, rows[half]]
             if c < 3:
-                for b in (0, 1):
-                    pltpu.make_async_remote_copy(hm.at[t, c, b * hl + h, halves[half]], dst, send_in, recv_in.at[h],
-                                                 device_id={'cp': peers[c][b]}, device_id_type=MESH).start()
+                go = me >= 0
+                if t in (1, 2) and half == 1:
+                    go = outer
+                if (t, c, h) in relayed:
+                    go = jnp.logical_and(go, chip != 2)
+
+                @pl.when(go)
+                def _():
+                    for b in (0, 1):
+                        pltpu.make_async_remote_copy(hm.at[t, c, b * hl + h, halves[half]], dst, send_in, recv_in.at[h],
+                                                     device_id={'cp': peers[c][b]}, device_id_type=MESH).start()
             else:
                 pltpu.make_async_remote_copy(hm.at[t, c, (1 - core) * hl + h, halves[half]], dst, send_in, recv_in.at[h],
                                              device_id={'cp': other}, device_id_type=MESH).start()
                 pltpu.make_async_copy(hm.at[t, c, core * hl + h, halves[half]], dst, recv_in.at[h]).start()
 
+    relayed = [(t, 2, hl - 1) for t in (0, 1)]
+
+    def forward():
+        pltpu.make_async_copy(rel, rel, rel_sem).wait()
+        for t in (0, 1):
+            for b in (0, 1):
+                for half, seg in ((0, me + 4), (1, NSEG - 5 - me)):
+                    dst = xin.at[hl - 1, t, pl.ds(pl.multiple_of(seg * SEG, SEG), SEG)]
+                    pltpu.make_async_remote_copy(rel.at[t, b, halves[half]], dst, fwd_sem, recv_in.at[hl - 1],
+                                                 device_id={'cp': 2 + b}, device_id_type=MESH).start()
+
+    @pl.when(outer)
+    def _():
+        for h in range(hl):
+            for t in (1, 2):
+                xin[h, t, last, :] = jnp.zeros((2 * SEG, xin.shape[-1]), BF16)
+
     for n, (t, c) in enumerate(units):
         if n + AHEAD < len(loads):
             loads[n + AHEAD].start()
         loads[n].wait()
-        _swap(hm.at[t, c], nat.at[t, c], tok)
+        _swap(hm.at[t, c], nat.at[n % RING], tok)
         if n == 0:
             pl.semaphore_wait(barrier, N - 1)
         else:
@@ -112,7 +138,7 @@
     load_lse.wait()
     for c in range(4):
         loads[16 + c].wait()
-        _swap(ohm, onat.at[c], tok)
+        _swap(ohm, nat.at[(16 + c) % RING], tok)
         if c == 0:
             send(*units[-1], 0)
         delta = jnp.zeros((2 * hl, tok), F32)
@@ -136,18 +162,85 @@
         pltpu.make_async_remote_copy(ldst.at[3, 1 - core, half], dst, send_ld, recv_ld,
                                      device_id={'cp': other}, device_id_type=MESH).start()
         pltpu.make_async_copy(ldst.at[3, core, half], dst, recv_ld).start()
+
+    @pl.when(chip == 2)
+    def _():
+        for t in (0, 1):
+            for b in (0, 1):
+                pltpu.make_async_remote_copy(hm.at[t, 2, b * hl + hl - 1], rel.at[t, b], send_in, rel_sem,
+                                             device_id={'cp': 2 * chips[1] + core}, device_id_type=MESH).start()
+
+    own_rows = pl.ds(pl.multiple_of((1 - core) * SEG, SEG), SEG)
+    other_rows = pl.ds(pl.multiple_of(core * SEG, SEG), SEG)
+    own_heads = pl.ds(core * hl, hl)
+    other_heads = pl.ds((1 - core) * hl, hl)
+
+    @pl.when(chip == 0)
+    def _():
+        for c in range(3):
+            for t in range(4):
+                dst = loc.at[c, t, :, own_rows]
+                pltpu.make_async_copy(hm.at[t, c, own_heads, halves[1]], dst, recv_loc.at[0]).start()
+                pltpu.make_async_remote_copy(hm.at[t, c, other_heads, halves[1]], dst, send_loc.at[0], recv_loc.at[0],
+                                             device_id={'cp': other}, device_id_type=MESH).start()
+            dst = locld.at[c, 1 - core]
+            pltpu.make_async_copy(ldst.at[c, core, 1], dst, recv_loc.at[1]).start()
+            pltpu.make_async_remote_copy(ldst.at[c, 1 - core, 1], dst, send_loc.at[1], recv_loc.at[1],
+                                         device_id={'cp': other}, device_id_type=MESH).start()
+
     for h in range(1, hl):
         for c in range(4):
             for t in range(4):
                 send(t, c, h)
 
+    @pl.when(chip == 0)
+    def _():
+        pltpu.make_async_copy(loc, loc, recv_loc.at[0]).wait()
+        pltpu.make_async_copy(locld, locld, recv_loc.at[1]).wait()
+
+        @pl.loop(0, 3 * hl)
+        def _(i):
+            c, h = i // hl, i % hl
+            qb, kb, vb, dob = (loc[c, t, h] for t in range(4))
+            l2 = jnp.concatenate([locld[c, s, pl.ds(h, 1), :] for s in (0, 1)], axis=1)
+            dl = jnp.concatenate([locld[c, s, pl.ds(hl + h, 1), :] for s in (0, 1)], axis=1)
+            p = jnp.exp2(_nt(kb, qb) * (scale * LOG2E) - l2)
+            key = lax.broadcasted_iota(jnp.int32, p.shape, 0)
+            query = lax.broadcasted_iota(jnp.int32, p.shape, 1)
+            p = jnp.where(key <= query, p, 0.0)
+            ds = (p * (_nt(vb, dob) - dl)).astype(BF16)
+            lkv[0, c, h] = (_nn(ds, qb) * scale).astype(BF16)
+            lkv[1, c, h] = _nn(p.astype(BF16), dob).astype(BF16)
+            ldq[c, h] = _tn(ds, kb)
+
+        for c in range(3):
+            heads = pl.ds((2 * chips[c] + core) * hl, hl)
+            for t in (0, 1):
+                dst = rin.at[t, heads, halves[1]]
+                pltpu.make_async_copy(lkv.at[t, c, :, own_rows], dst, recv_out.at[t + 1]).start()
+                pltpu.make_async_remote_copy(lkv.at[t, c, :, other_rows], dst, send_loc.at[2], recv_out.at[t + 1],
+                                             device_id={'cp': other}, device_id_type=MESH).start()
+            dst = gdq.at[c, core]
+            pltpu.make_async_copy(ldq.at[c, :, own_rows], dst, gdq_sem).start()
+            pltpu.make_async_remote_copy(ldq.at[c, :, other_rows], dst, send_loc.at[3], gdq_sem,
+                                         device_id={'cp': other}, device_id_type=MESH).start()
+
     pltpu.make_async_copy(ldin, ldin, recv_ld).wait()
 
     nblk = NSEG * SEG // BLK
     per = BLK // SEG
+    keys = jnp.where(outer, BLK - 2 * SEG, BLK)
 
     def head(h, carry):
-        pltpu.make_async_copy(xin.at[h], xin.at[h], recv_in.at[h]).wait()
+        @pl.when(outer)
+        def _():
+            most = xin.at[h, :, pl.ds(0, (NSEG - 1) * SEG)]
+            pltpu.make_async_copy(most, most, recv_in.at[h]).wait()
+
+        @pl.when(chip == 0)
+        def _():
+            pltpu.make_async_copy(xin.at[h], xin.at[h], recv_in.at[h]).wait()
+
         dqacc[...] = jnp.zeros_like(dqacc)
 
         for j in range(nblk):
@@ -163,7 +256,10 @@
                 if masked:
                     key = lax.broadcasted_iota(jnp.int32, (BLK, BLK), 0)
                     query = lax.broadcasted_iota(jnp.int32, (BLK, BLK), 1)
-                    p = jnp.where(key <= query, p, 0.0)
+                    seen = key <= query
+                    if j == nblk - 1:
+                        seen = jnp.logical_and(seen, key < keys)
+                    p = jnp.where(seen, p, 0.0)
                 ds = (p * (_nt(vb, dob) - dl)).astype(BF16)
                 dvb = _nn(p.astype(BF16), dob)
                 dkb = _nn(ds, qb)
@@ -184,13 +280,30 @@
             obuf[h, 2, kr, :] = dvacc[...].astype(BF16)
         obuf[h, 0] = (dqacc[...] * scale).astype(BF16)
 
+        @pl.when(outer)
+        def _():
+            fdq[h] = dqacc[last, :]
+            for b in (0, 1):
+                pltpu.make_async_remote_copy(fdq.at[h, pl.ds((1 - b) * SEG, SEG)], rdq.at[chip - 1, core, h], send_fdq, rdq_sem,
+                                             device_id={'cp': b}, device_id_type=MESH).start()
+
+        @pl.when(jnp.logical_and(chip == 0, h == 0))
+        def _():
+            forward()
+
         mine = me * hl + h
         for t, x in ((1, rin.at[0]), (2, rin.at[1]), (0, dqh)):
             for p in remote:
                 for half, seg in ((0, p), (1, NSEG - 1 - p)):
                     src = obuf.at[h, t, pl.ds(pl.multiple_of(seg * SEG, SEG), SEG)]
-                    pltpu.make_async_remote_copy(src, x.at[mine, halves[half]], send_out, recv_out.at[t],
-                                                 device_id={'cp': p}, device_id_type=MESH).start()
+                    go = me >= 0
+                    if half == 1:
+                        go = jnp.logical_not(jnp.logical_and(outer, p < 2))
+
+                    @pl.when(go)
+                    def _():
+                        pltpu.make_async_remote_copy(src, x.at[mine, halves[half]], send_out, recv_out.at[t],
+                                                     device_id={'cp': p}, device_id_type=MESH).start()
             for half in (0, 1):
                 pltpu.make_async_copy(obuf.at[h, t, rows[half]], x.at[mine, halves[half]], recv_out.at[t]).start()
         return carry
@@ -203,11 +316,38 @@
         for g in range(N // 2):
             heads = pl.ds(g * 2 * hl, 2 * hl)
             _swap(x.at[:, heads], src.at[heads], tok, inverse=True)
-    pltpu.make_async_copy(dqh, dqh, recv_out.at[0]).wait()
-    far = pl.ds(0, (N - 1) * NSEG * SEG // N)
+
+    @pl.when(chip == 0)
+    def _():
+        pltpu.make_async_copy(gdq, gdq, gdq_sem).wait()
+        pltpu.make_async_copy(rdq, rdq, rdq_sem).wait()
+
+        @pl.loop(0, 6 * hl)
+        def _(i):
+            c, r = i // (2 * hl), i % (2 * hl)
+            total = gdq[c, r // hl, r % hl] + rdq[c, r // hl, r % hl]
+            dqh[2 * hl + i, halves[1], :] = (total * scale).astype(BF16)
+
+        some = dqh.at[pl.ds(0, 5 * hl)]
+        pltpu.make_async_copy(some, some, recv_out.at[0]).wait()
+        for n, ref in enumerate((loc.at[:, :, :, halves[0]], locld.at[:, 0], lkv.at[:, :, :, halves[0]], ldq.at[:, :, halves[0]])):
+            pltpu.make_async_copy(ref, ref, send_loc.at[n]).wait()
+        pltpu.make_async_copy(rel, rel, fwd_sem).wait()
+        sent = xin.at[:, :, pl.ds(0, 11 * SEG)]
+        pltpu.make_async_copy(sent, sent, send_in).wait()
+        sent = obuf.at[:, :, pl.ds(0, 14 * SEG)]
+        pltpu.make_async_copy(sent, sent, send_out).wait()
+
+    @pl.when(outer)
+    def _():
+        pltpu.make_async_copy(dqh, dqh, recv_out.at[0]).wait()
+        pltpu.make_async_copy(fdq, fdq, send_fdq).wait()
+        sent = xin.at[:, :, pl.ds(0, 14 * SEG)]
+        pltpu.make_async_copy(sent, sent, send_in).wait()
+        sent = obuf.at[:, :, pl.ds(0, 12 * SEG)]
+        pltpu.make_async_copy(sent, sent, send_out).wait()
+
     pltpu.make_async_copy(ldin.at[pl.ds(0, 2 * (N - 1))], ldin.at[pl.ds(0, 2 * (N - 1))], send_ld).wait()
-    pltpu.make_async_copy(xin.at[:, :, far], xin.at[:, :, far], send_in).wait()
-    pltpu.make_async_copy(obuf.at[:, :, far], obuf.at[:, :, far], send_out).wait()
 
 
 def _close(dqh, dkt, dvt, dq, dk, dv, dqt, sem):
@@ -240,8 +380,7 @@
             in_specs=[any_] * 6,
             out_specs=[vmem] * 3,
             scratch_shapes=[
-                pltpu.VMEM((4, N // 2, tok, 2 * hl, dim), BF16),
-                pltpu.VMEM((N // 2, tok, 2 * hl, dim), BF16),
+                pltpu.VMEM((RING, tok, 2 * hl, dim), BF16),
                 pltpu.VMEM((heads, tok), F32),
                 pltpu.VMEM((4, N // 2, 2 * hl, tok, dim), BF16),
                 pltpu.VMEM((2 * hl, tok, dim), BF16),
@@ -253,7 +392,15 @@
                 pltpu.VMEM((seq, dim), F32),
                 pltpu.VMEM((BLK, dim), F32),
                 pltpu.VMEM((BLK, dim), F32),
-                pltpu.SemaphoreType.DMA((5, N // 2)),
+                pltpu.VMEM((2, 2, tok, dim), BF16),
+                pltpu.VMEM((3, 4, hl, 2 * SEG, dim), BF16),
+                pltpu.VMEM((3, 2, 2 * hl, SEG), F32),
+                pltpu.VMEM((2, 3, hl, 2 * SEG, dim), BF16),
+                pltpu.VMEM((3, hl, 2 * SEG, dim), F32),
+                pltpu.VMEM((3, 2, hl, SEG, dim), F32),
+                pltpu.VMEM((3, 2, hl, SEG, dim), F32),
+                pltpu.VMEM((hl, 2 * SEG, dim), F32),
+                pltpu.SemaphoreType.DMA((RING,)),
                 pltpu.SemaphoreType.DMA,
                 pltpu.SemaphoreType.DMA,
                 pltpu.SemaphoreType.DMA((hl,)),
@@ -261,6 +408,13 @@
                 pltpu.SemaphoreType.DMA,
                 pltpu.SemaphoreType.DMA,
                 pltpu.SemaphoreType.DMA((3,)),
+                pltpu.SemaphoreType.DMA,
+                pltpu.SemaphoreType.DMA,
+                pltpu.SemaphoreType.DMA((4,)),
+                pltpu.SemaphoreType.DMA((2,)),
+                pltpu.SemaphoreType.DMA,
+                pltpu.SemaphoreType.DMA,
+                pltpu.SemaphoreType.DMA,
             ],
             compiler_params=pltpu.CompilerParams(collective_id=0, has_side_effects=True,
                                                  vmem_limit_bytes=46 * 2 ** 20),

time: 168 us -> 163 us (0.970)
  Pallas kernels: 167 us -> 161 us
    pallas_call x1, Pallas kernels: 164 us -> 158 us  [local(): pl.pallas_call(functools.partial(_kernel, hl, dim ** (-0.5)), out_shape=[...]
where the time goes in v4:
time: 163 us; the launch traced here: 162 us
  Pallas kernels  161 us (99%)
    pallas_call x1, Pallas kernels, local(): pl.pallas_call(functools.partial(_kernel, hl, dim ** (-0.5)), out_shape=[...  158 us

profile of v4, /device:TPU:1, one launch (start us, length us, event | category | flops | bytes accessed | tf_op | source)
XLA Modules:
  0.0 162.2 jit_solution(8020093355717431168)
XLA Ops:
  0.6 0.0 copy-start
  0.6 0.7 copy-done
  1.4 158.1 %attention_backward.1 = (bf16[32,256,128]{2,1,0:T(8,128)(2,1)S(1)}, bf16[256,32,128]{2,1,0:T(8,128)(2,1)S(1)}, bf16[256,32,128]{2,1,0:T(8,128)(2,1)S(1)}) custom-call(bf16[256,32,128]{2,1,0:T(8,128)(2,1)} %bitcast.10, bf16[256,32,128]{2,1,0:T(8,128)(2,1)} %bitcast.11, bf16[256,32,128]{2,1,0:T(8,128)(2,1)} %bitcast.12, bf16[256,32,128]{2,1,0:T(8,128)(2,1)} %bitcast.13, ...), custom_call_target="tpu_custom_call" | custom-call | tf_op jit(solution)/shard_map/attention_backward/pallas_call | solution.py:377
  159.5 2.7 %close.1 = (bf16[256,32,128]{2,1,0:T(8,128)(2,1)}, bf16[256,32,128]{2,1,0:T(8,128)(2,1)}, bf16[256,32,128]{2,1,0:T(8,128)(2,1)}) custom-call(bf16[32,256,128]{2,1,0:T(8,128)(2,1)S(1)} %get-tuple-element.9.dqh, bf16[256,32,128]{2,1,0:T(8,128)(2,1)S(1)} %get-tuple-element.10.dkt, bf16[256,32,128]{2,1,0:T(8,128)(2,1)S(1)} %get-tuple-element.11.dvt), custom_call_target="tpu_custom_call" | custom-call | tf_op jit(solution)/shard_map/close/pallas_call | solution.py:423
Async XLA Ops:
  0.6 0.8 copy-start

commit v5 on v4

--- a/solution.py
+++ b/solution.py
@@ -54,15 +54,16 @@
 
 
 def _kernel(hl, scale, q, k, v, do, o, lse, dqh, dk, dv, nat, lsev, hm, ohm, ldst, xin, ldin, obuf, rin,
-            dqacc, dkacc, dvacc, rel, loc, locld, lkv, ldq, gdq, rdq, fdq,
+            dqacc, dkacc, dvacc, rel, loc, locld, lkv, ldq, gdq, rdq, fdq, pdq,
             nat_sem, lse_sem, send_in, recv_in, send_ld, recv_ld, send_out, recv_out,
-            rel_sem, fwd_sem, send_loc, recv_loc, gdq_sem, send_fdq, rdq_sem):
+            rel_sem, fwd_sem, send_loc, recv_loc, gdq_sem, send_fdq, rdq_sem, pdq_sem, send_pdq):
     me = lax.axis_index('cp')
     core = me % 2
     chip = me // 2
     chips = [_chip(chip, f) for f in CHIPS]
     tok = nat.shape[1]
     outer = chip != 0
+    first = pl.ds(0, hl - 1)
     last = pl.ds((NSEG - 2) * SEG, 2 * SEG)
     peers = [[2 * chip + b for b in (0, 1)] for chip in chips]
     other = me + 1 - 2 * core
@@ -91,15 +92,13 @@
         for half in (0, 1):
             dst = xin.at[h, t, rows[half]]
             if c < 3:
-                go = me >= 0
-                if t in (1, 2) and half == 1:
-                    go = outer
-                if (t, c, h) in relayed:
-                    go = jnp.logical_and(go, chip != 2)
-
-                @pl.when(go)
-                def _():
-                    for b in (0, 1):
+                for b in (0, 1):
+                    go = outer if t in (1, 2) and half == 1 else me >= 0
+                    if c == 2 and h == hl - 1 and (t, b) in relayed:
+                        go = jnp.logical_and(go, chip != 2)
+
+                    @pl.when(go)
+                    def _():
                         pltpu.make_async_remote_copy(hm.at[t, c, b * hl + h, halves[half]], dst, send_in, recv_in.at[h],
                                                      device_id={'cp': peers[c][b]}, device_id_type=MESH).start()
             else:
@@ -107,16 +106,15 @@
                                              device_id={'cp': other}, device_id_type=MESH).start()
                 pltpu.make_async_copy(hm.at[t, c, core * hl + h, halves[half]], dst, recv_in.at[h]).start()
 
-    relayed = [(t, 2, hl - 1) for t in (0, 1)]
+    relayed = [(0, 0), (0, 1), (1, 0), (1, 1), (2, 0)]
 
     def forward():
         pltpu.make_async_copy(rel, rel, rel_sem).wait()
-        for t in (0, 1):
-            for b in (0, 1):
-                for half, seg in ((0, me + 4), (1, NSEG - 5 - me)):
-                    dst = xin.at[hl - 1, t, pl.ds(pl.multiple_of(seg * SEG, SEG), SEG)]
-                    pltpu.make_async_remote_copy(rel.at[t, b, halves[half]], dst, fwd_sem, recv_in.at[hl - 1],
-                                                 device_id={'cp': 2 + b}, device_id_type=MESH).start()
+        for n, (t, b) in enumerate(relayed):
+            for half, seg in ((0, me + 4), (1, NSEG - 5 - me)):
+                dst = xin.at[hl - 1, t, pl.ds(pl.multiple_of(seg * SEG, SEG), SEG)]
+                pltpu.make_async_remote_copy(rel.at[n, halves[half]], dst, fwd_sem, recv_in.at[hl - 1],
+                                             device_id={'cp': 2 + b}, device_id_type=MESH).start()
 
     @pl.when(outer)
     def _():
@@ -165,10 +163,9 @@
 
     @pl.when(chip == 2)
     def _():
-        for t in (0, 1):
-            for b in (0, 1):
-                pltpu.make_async_remote_copy(hm.at[t, 2, b * hl + hl - 1], rel.at[t, b], send_in, rel_sem,
-                                             device_id={'cp': 2 * chips[1] + core}, device_id_type=MESH).start()
+        for n, (t, b) in enumerate(relayed):
+            pltpu.make_async_remote_copy(hm.at[t, 2, b * hl + hl - 1], rel.at[n], send_in, rel_sem,
+                                         device_id={'cp': 2 * chips[1] + core}, device_id_type=MESH).start()
 
     own_rows = pl.ds(pl.multiple_of((1 - core) * SEG, SEG), SEG)
     other_rows = pl.ds(pl.multiple_of(core * SEG, SEG), SEG)
@@ -221,9 +218,11 @@
                 pltpu.make_async_remote_copy(lkv.at[t, c, :, other_rows], dst, send_loc.at[2], recv_out.at[t + 1],
                                              device_id={'cp': other}, device_id_type=MESH).start()
             dst = gdq.at[c, core]
-            pltpu.make_async_copy(ldq.at[c, :, own_rows], dst, gdq_sem).start()
-            pltpu.make_async_remote_copy(ldq.at[c, :, other_rows], dst, send_loc.at[3], gdq_sem,
+            pltpu.make_async_copy(ldq.at[c, first, own_rows], dst, gdq_sem).start()
+            pltpu.make_async_remote_copy(ldq.at[c, first, other_rows], dst, send_loc.at[3], gdq_sem,
                                          device_id={'cp': other}, device_id_type=MESH).start()
+            pltpu.make_async_remote_copy(ldq.at[c, hl - 1], pdq, send_pdq, pdq_sem,
+                                         device_id={'cp': peers[c][0] + core}, device_id_type=MESH).start()
 
     pltpu.make_async_copy(ldin, ldin, recv_ld).wait()
 
@@ -278,9 +277,15 @@
 
             obuf[h, 1, kr, :] = (dkacc[...] * scale).astype(BF16)
             obuf[h, 2, kr, :] = dvacc[...].astype(BF16)
+
+        @pl.when(jnp.logical_and(outer, h == hl - 1))
+        def _():
+            pltpu.make_async_copy(pdq, pdq, pdq_sem).wait()
+            dqacc[last, :] += pdq[...]
+
         obuf[h, 0] = (dqacc[...] * scale).astype(BF16)
 
-        @pl.when(outer)
+        @pl.when(jnp.logical_and(outer, h < hl - 1))
         def _():
             fdq[h] = dqacc[last, :]
             for b in (0, 1):
@@ -304,6 +309,12 @@
                     def _():
                         pltpu.make_async_remote_copy(src, x.at[mine, halves[half]], send_out, recv_out.at[t],
                                                      device_id={'cp': p}, device_id_type=MESH).start()
+
+                    if half == 1 and t == 0:
+                        @pl.when(jnp.logical_and(jnp.logical_not(go), h == hl - 1))
+                        def _():
+                            pltpu.make_async_remote_copy(src, x.at[mine, halves[half]], send_pdq, recv_out.at[t],
+                                                         device_id={'cp': p}, device_id_type=MESH).start()
             for half in (0, 1):
                 pltpu.make_async_copy(obuf.at[h, t, rows[half]], x.at[mine, halves[half]], recv_out.at[t]).start()
         return carry
@@ -322,15 +333,18 @@
         pltpu.make_async_copy(gdq, gdq, gdq_sem).wait()
         pltpu.make_async_copy(rdq, rdq, rdq_sem).wait()
 
-        @pl.loop(0, 6 * hl)
+        few = hl - 1
+
+        @pl.loop(0, 6 * few)
         def _(i):
-            c, r = i // (2 * hl), i % (2 * hl)
-            total = gdq[c, r // hl, r % hl] + rdq[c, r // hl, r % hl]
-            dqh[2 * hl + i, halves[1], :] = (total * scale).astype(BF16)
-
-        some = dqh.at[pl.ds(0, 5 * hl)]
+            c, b, h = i // (2 * few), (i // few) % 2, i % few
+            total = gdq[c, b, h] + rdq[c, b, h]
+            dqh[(2 * c + 2 + b) * hl + h, halves[1], :] = (total * scale).astype(BF16)
+
+        some = dqh.at[pl.ds(0, 2 * N * hl // 2 - 3 * few)]
         pltpu.make_async_copy(some, some, recv_out.at[0]).wait()
-        for n, ref in enumerate((loc.at[:, :, :, halves[0]], locld.at[:, 0], lkv.at[:, :, :, halves[0]], ldq.at[:, :, halves[0]])):
+        pltpu.make_async_copy(ldq.at[:, hl - 1], ldq.at[:, hl - 1], send_pdq).wait()
+        for n, ref in enumerate((loc.at[:, :, :, halves[0]], locld.at[:, 0], lkv.at[:, :, :, halves[0]], ldq.at[:, first, halves[0]])):
             pltpu.make_async_copy(ref, ref, send_loc.at[n]).wait()
         pltpu.make_async_copy(rel, rel, fwd_sem).wait()
         sent = xin.at[:, :, pl.ds(0, 11 * SEG)]
@@ -342,6 +356,8 @@
     def _():
         pltpu.make_async_copy(dqh, dqh, recv_out.at[0]).wait()
         pltpu.make_async_copy(fdq, fdq, send_fdq).wait()
+        sent = obuf.at[hl - 1, 0, last]
+        pltpu.make_async_copy(sent, sent, send_pdq).wait()
         sent = xin.at[:, :, pl.ds(0, 14 * SEG)]
         pltpu.make_async_copy(sent, sent, send_in).wait()
         sent = obuf.at[:, :, pl.ds(0, 12 * SEG)]
@@ -392,14 +408,15 @@
                 pltpu.VMEM((seq, dim), F32),
                 pltpu.VMEM((BLK, dim), F32),
                 pltpu.VMEM((BLK, dim), F32),
-                pltpu.VMEM((2, 2, tok, dim), BF16),
+                pltpu.VMEM((5, tok, dim), BF16),
                 pltpu.VMEM((3, 4, hl, 2 * SEG, dim), BF16),
                 pltpu.VMEM((3, 2, 2 * hl, SEG), F32),
                 pltpu.VMEM((2, 3, hl, 2 * SEG, dim), BF16),
                 pltpu.VMEM((3, hl, 2 * SEG, dim), F32),
-                pltpu.VMEM((3, 2, hl, SEG, dim), F32),
-                pltpu.VMEM((3, 2, hl, SEG, dim), F32),
-                pltpu.VMEM((hl, 2 * SEG, dim), F32),
+                pltpu.VMEM((3, 2, hl - 1, SEG, dim), F32),
+                pltpu.VMEM((3, 2, hl - 1, SEG, dim), F32),
+                pltpu.VMEM((hl - 1, 2 * SEG, dim), F32),
+                pltpu.VMEM((2 * SEG, dim), F32),
                 pltpu.SemaphoreType.DMA((RING,)),
                 pltpu.SemaphoreType.DMA,
                 pltpu.SemaphoreType.DMA,
@@ -412,6 +429,8 @@
                 pltpu.SemaphoreType.DMA,
                 pltpu.SemaphoreType.DMA((4,)),
                 pltpu.SemaphoreType.DMA((2,)),
+                pltpu.SemaphoreType.DMA,
+                pltpu.SemaphoreType.DMA,
                 pltpu.SemaphoreType.DMA,
                 pltpu.SemaphoreType.DMA,
                 pltpu.SemaphoreType.DMA,

time: 163 us -> 161 us (0.988)
  no operation moved by 1% of the time
where the time goes in v5:
time: 161 us
  Pallas kernels  160 us (99%)
    pallas_call x1, Pallas kernels, local(): pl.pallas_call(functools.partial(_kernel, hl, dim ** (-0.5)), out_shape=[...  157 us

profile of v5, /device:TPU:1, one launch (start us, length us, event | category | flops | bytes accessed | tf_op | source)
XLA Modules:
  0.0 161.1 jit_solution(16410743118874576296)
XLA Ops:
  0.6 0.0 copy-start
  0.6 0.7 copy-done
  1.4 157.0 %attention_backward.1 = (bf16[32,256,128]{2,1,0:T(8,128)(2,1)S(1)}, bf16[256,32,128]{2,1,0:T(8,128)(2,1)S(1)}, bf16[256,32,128]{2,1,0:T(8,128)(2,1)S(1)}) custom-call(bf16[256,32,128]{2,1,0:T(8,128)(2,1)} %bitcast.10, bf16[256,32,128]{2,1,0:T(8,128)(2,1)} %bitcast.11, bf16[256,32,128]{2,1,0:T(8,128)(2,1)} %bitcast.12, bf16[256,32,128]{2,1,0:T(8,128)(2,1)} %bitcast.13, ...), custom_call_target="tpu_custom_call" | custom-call | tf_op jit(solution)/shard_map/attention_backward/pallas_call | solution.py:393
  158.4 2.7 %close.1 = (bf16[256,32,128]{2,1,0:T(8,128)(2,1)}, bf16[256,32,128]{2,1,0:T(8,128)(2,1)}, bf16[256,32,128]{2,1,0:T(8,128)(2,1)}) custom-call(bf16[32,256,128]{2,1,0:T(8,128)(2,1)S(1)} %get-tuple-element.9.dqh, bf16[256,32,128]{2,1,0:T(8,128)(2,1)S(1)} %get-tuple-element.10.dkt, bf16[256,32,128]{2,1,0:T(8,128)(2,1)S(1)} %get-tuple-element.11.dvt), custom_call_target="tpu_custom_call" | custom-call | tf_op jit(solution)/shard_map/close/pallas_call | solution.py:442
Async XLA Ops:
  0.6 0.8 copy-start

commit v6 on v5

--- a/solution.py
+++ b/solution.py
@@ -67,7 +67,7 @@
     last = pl.ds((NSEG - 2) * SEG, 2 * SEG)
     peers = [[2 * chip + b for b in (0, 1)] for chip in chips]
     other = me + 1 - 2 * core
-    remote = [p for ps in peers[:3] for p in ps] + [other]
+    remote = [p for c in (2, 1, 0) for p in peers[c]] + [other]
 
     barrier = pltpu.get_barrier_semaphore()
     for p in remote:
@@ -127,9 +127,11 @@
             loads[n + AHEAD].start()
         loads[n].wait()
         _swap(hm.at[t, c], nat.at[n % RING], tok)
-        if n == 0:
+        if n == 3:
             pl.semaphore_wait(barrier, N - 1)
-        else:
+            for unit in units[:n]:
+                send(*unit, 0)
+        elif n > 3:
             send(*units[n - 1], 0)
 
     row = lax.broadcasted_iota(jnp.int32, (2 * hl, nat.shape[-1]), 0)
@@ -186,8 +188,8 @@
                                          device_id={'cp': other}, device_id_type=MESH).start()
 
     for h in range(1, hl):
-        for c in range(4):
-            for t in range(4):
+        for t in range(4):
+            for c in (2, 1, 0, 3):
                 send(t, c, h)
 
     @pl.when(chip == 0)

time: 161 us -> 161 us (level)
  no operation moved by 1% of the time
where the time goes in v6:
time: 161 us; the launch traced here: 160 us
  Pallas kernels  159 us (99%)
    pallas_call x1, Pallas kernels, local(): pl.pallas_call(functools.partial(_kernel, hl, dim ** (-0.5)), out_shape=[...  156 us

profile of v6, /device:TPU:1, one launch (start us, length us, event | category | flops | bytes accessed | tf_op | source)
XLA Modules:
  0.0 160.3 jit_solution(7363787844296274580)
XLA Ops:
  0.6 0.0 copy-start
  0.6 0.7 copy-done
  1.4 156.2 %attention_backward.1 = (bf16[32,256,128]{2,1,0:T(8,128)(2,1)S(1)}, bf16[256,32,128]{2,1,0:T(8,128)(2,1)S(1)}, bf16[256,32,128]{2,1,0:T(8,128)(2,1)S(1)}) custom-call(bf16[256,32,128]{2,1,0:T(8,128)(2,1)} %bitcast.10, bf16[256,32,128]{2,1,0:T(8,128)(2,1)} %bitcast.11, bf16[256,32,128]{2,1,0:T(8,128)(2,1)} %bitcast.12, bf16[256,32,128]{2,1,0:T(8,128)(2,1)} %bitcast.13, ...), custom_call_target="tpu_custom_call" | custom-call | tf_op jit(solution)/shard_map/attention_backward/pallas_call | solution.py:395
  157.6 2.7 %close.1 = (bf16[256,32,128]{2,1,0:T(8,128)(2,1)}, bf16[256,32,128]{2,1,0:T(8,128)(2,1)}, bf16[256,32,128]{2,1,0:T(8,128)(2,1)}) custom-call(bf16[32,256,128]{2,1,0:T(8,128)(2,1)S(1)} %get-tuple-element.9.dqh, bf16[256,32,128]{2,1,0:T(8,128)(2,1)S(1)} %get-tuple-element.10.dkt, bf16[256,32,128]{2,1,0:T(8,128)(2,1)S(1)} %get-tuple-element.11.dvt), custom_call_target="tpu_custom_call" | custom-call | tf_op jit(solution)/shard_map/close/pallas_call | solution.py:444
Async XLA Ops:
  0.6 0.8 copy-start

commit v7 on v6

--- a/solution.py
+++ b/solution.py
@@ -143,7 +143,7 @@
             send(*units[-1], 0)
         delta = jnp.zeros((2 * hl, tok), F32)
         for g in range(2 * hl):
-            prod = hm[3, c, g].astype(F32) * ohm[g].astype(F32)
+            prod = (0.5 * hm[3, c, g].astype(F32)) * ohm[g].astype(F32)
             top = prod.astype(BF16)
             low = (prod - top.astype(F32)).astype(BF16)
             pick = jnp.where(row == g, 1.0, 0.0).astype(BF16)
@@ -152,7 +152,7 @@
         for b in (0, 1):
             for half in (0, 1):
                 ldst[c, b, half, 0:hl, :] = l2[b * hl:(b + 1) * hl, half * SEG:(half + 1) * SEG]
-                ldst[c, b, half, hl:2 * hl, :] = delta[b * hl:(b + 1) * hl, half * SEG:(half + 1) * SEG]
+                ldst[c, b, half, hl:2 * hl, :] = 2.0 * delta[b * hl:(b + 1) * hl, half * SEG:(half + 1) * SEG]
     for half in (0, 1):
         dst = ldin.at[segs[half]]
         for c in range(3):

time: 161 us -> 161 us (level)
  no operation moved by 1% of the time
where the time goes in v7:
time: 161 us; the launch traced here: 160 us
  Pallas kernels  159 us (99%)
    pallas_call x1, Pallas kernels, local(): pl.pallas_call(functools.partial(_kernel, hl, dim ** (-0.5)), out_shape=[...  156 us

profile of v7, /device:TPU:1, one launch (start us, length us, event | category | flops | bytes accessed | tf_op | source)
XLA Modules:
  0.0 160.3 jit_solution(658944331965261164)
XLA Ops:
  0.6 0.0 copy-start
  0.6 0.7 copy-done
  1.4 156.2 %attention_backward.1 = (bf16[32,256,128]{2,1,0:T(8,128)(2,1)S(1)}, bf16[256,32,128]{2,1,0:T(8,128)(2,1)S(1)}, bf16[256,32,128]{2,1,0:T(8,128)(2,1)S(1)}) custom-call(bf16[256,32,128]{2,1,0:T(8,128)(2,1)} %bitcast.10, bf16[256,32,128]{2,1,0:T(8,128)(2,1)} %bitcast.11, bf16[256,32,128]{2,1,0:T(8,128)(2,1)} %bitcast.12, bf16[256,32,128]{2,1,0:T(8,128)(2,1)} %bitcast.13, ...), custom_call_target="tpu_custom_call" | custom-call | tf_op jit(solution)/shard_map/attention_backward/pallas_call | solution.py:395
  157.6 2.7 %close.1 = (bf16[256,32,128]{2,1,0:T(8,128)(2,1)}, bf16[256,32,128]{2,1,0:T(8,128)(2,1)}, bf16[256,32,128]{2,1,0:T(8,128)(2,1)}) custom-call(bf16[32,256,128]{2,1,0:T(8,128)(2,1)S(1)} %get-tuple-element.9.dqh, bf16[256,32,128]{2,1,0:T(8,128)(2,1)S(1)} %get-tuple-element.10.dkt, bf16[256,32,128]{2,1,0:T(8,128)(2,1)S(1)} %get-tuple-element.11.dvt), custom_call_target="tpu_custom_call" | custom-call | tf_op jit(solution)/shard_map/close/pallas_call | solution.py:444
Async XLA Ops:
  0.6 0.8 copy-start

commit v8 on v7

--- a/solution.py
+++ b/solution.py
@@ -369,14 +369,17 @@
 
 
 def _close(dqh, dkt, dvt, dq, dk, dv, dqt, sem):
-    copies = [pltpu.make_async_copy(dkt, dk, sem.at[0]), pltpu.make_async_copy(dvt, dv, sem.at[1])]
+    heads, tok = dqh.shape[:2]
+    parts = [pl.ds(i * CHUNK, CHUNK) for i in range(tok // CHUNK)]
+    copies = [pltpu.make_async_copy(x.at[r], y.at[r], sem.at[n, i])
+              for n, (x, y) in enumerate(((dkt, dk), (dvt, dv))) for i, r in enumerate(parts)]
     for copy in copies:
         copy.start()
-    heads, tok = dqh.shape[:2]
-    for g in range(heads // 8):
-        part = pl.ds(g * 8, 8)
-        _swap(dqt.at[g], dqh.at[part], tok, inverse=True)
-        copies.append(pltpu.make_async_copy(dqt.at[g], dq.at[:, part], sem.at[2 + g]))
+    for i, r in enumerate(parts):
+        for g in range(heads // 8):
+            part = slice(g * 8, g * 8 + 8)
+            dqt[i, :, part, :] = jnp.swapaxes(dqh[part, r, :], 0, 1)
+        copies.append(pltpu.make_async_copy(dqt.at[i], dq.at[r], sem.at[2, i]))
         copies[-1].start()
     for copy in copies:
         copy.wait()
@@ -446,8 +449,8 @@
             out_shape=[jax.ShapeDtypeStruct((tok, heads, dim), BF16)] * 3,
             in_specs=[vmem] * 3,
             out_specs=[any_] * 3,
-            scratch_shapes=[pltpu.VMEM((heads // 8, tok, 8, dim), BF16),
-                            pltpu.SemaphoreType.DMA((2 + heads // 8,))],
+            scratch_shapes=[pltpu.VMEM((tok // CHUNK, CHUNK, heads, dim), BF16),
+                            pltpu.SemaphoreType.DMA((3, tok // CHUNK))],
             compiler_params=pltpu.CompilerParams(vmem_limit_bytes=16 * 2 ** 20),
             name='close',
         )(*outs)

time: 161 us -> 161 us (level)
  no operation moved by 1% of the time
where the time goes in v8:
time: 161 us; the launch traced here: 160 us
  Pallas kernels  159 us (99%)
    pallas_call x1, Pallas kernels, local(): pl.pallas_call(functools.partial(_kernel, hl, dim ** (-0.5)), out_shape=[...  156 us

profile of v8, /device:TPU:1, one launch (start us, length us, event | category | flops | bytes accessed | tf_op | source)
XLA Modules:
  0.0 160.3 jit_solution(9318777977583538687)
XLA Ops:
  0.6 0.0 copy-start
  0.6 0.7 copy-done
  1.4 156.2 %attention_backward.1 = (bf16[32,256,128]{2,1,0:T(8,128)(2,1)S(1)}, bf16[256,32,128]{2,1,0:T(8,128)(2,1)S(1)}, bf16[256,32,128]{2,1,0:T(8,128)(2,1)S(1)}) custom-call(bf16[256,32,128]{2,1,0:T(8,128)(2,1)} %bitcast.10, bf16[256,32,128]{2,1,0:T(8,128)(2,1)} %bitcast.11, bf16[256,32,128]{2,1,0:T(8,128)(2,1)} %bitcast.12, bf16[256,32,128]{2,1,0:T(8,128)(2,1)} %bitcast.13, ...), custom_call_target="tpu_custom_call" | custom-call | tf_op jit(solution)/shard_map/attention_backward/pallas_call | solution.py:398
  157.6 2.8 %close.1 = (bf16[256,32,128]{2,1,0:T(8,128)(2,1)}, bf16[256,32,128]{2,1,0:T(8,128)(2,1)}, bf16[256,32,128]{2,1,0:T(8,128)(2,1)}) custom-call(bf16[32,256,128]{2,1,0:T(8,128)(2,1)S(1)} %get-tuple-element.9.dqh, bf16[256,32,128]{2,1,0:T(8,128)(2,1)S(1)} %get-tuple-element.10.dkt, bf16[256,32,128]{2,1,0:T(8,128)(2,1)S(1)} %get-tuple-element.11.dvt), custom_call_target="tpu_custom_call" | custom-call | tf_op jit(solution)/shard_map/close/pallas_call | solution.py:447
Async XLA Ops:
  0.6 0.8 copy-start
